TPU v7x, 128 devices: a whole 4x4x4 slice. The times are simulated.
128 devices in a mesh: ctx: 32 (over y, z, core), mp: 4 (over x).
Axes of the slice: x: 4, y: 4, z: 4, core: 2. Of those that a mesh axis runs over, the one named last changes fastest.
Arguments:
- queries: bfloat16 [65536, 2048], P('ctx', 'mp'), may hold values from -6 to 6
- key_vectors: bfloat16 [65536, 2048], P('ctx', 'mp'), may hold values from -6 to 6
- value_vectors: bfloat16 [65536, 2048], P('ctx', 'mp'), may hold values from -6 to 6
- level_index: int32 [65536], P('ctx'), may hold values from 0 to 15
- level_table: float32 [16, 16, 20], P(None, 'mp'), may hold values from 0.1 to 4
- out_weight: bfloat16 [2048, 2048], P('mp'), may hold values from -0.125 to 0.125
Outputs:
- layer_out: bfloat16 [65536, 2048], P(('ctx', 'mp'))
All inputs are finite; a program needn't handle non-finite values.
Results may differ from a plain program's by a relative error of at most 0.015.
Values may be sent and summed in bfloat16 or wider, within the bound.
A program may use at most 128 MiB of HBM per device.

v0:
```python
import jax
import jax.numpy as jnp
from jax import lax
from jax.sharding import PartitionSpec as P

STRETCH = 256


EPSILON = 1e-06


def fenwick_level(offsets, digits):
    counted = jnp.zeros(offsets.shape, jnp.int32)
    for bit_index in range(digits):
        counted = counted + (offsets >= 1 << bit_index).astype(jnp.int32)
    return counted


def body(queries, key_vectors, value_vectors, level_index, level_table, out_weight):
    tok_rows = queries.shape[0]
    plans = level_table.shape[0]
    heads_here = level_table.shape[1]
    level_total = level_table.shape[2]
    head_size = queries.shape[1] // heads_here
    stretch_count = tok_rows // STRETCH
    stretch_bits = STRETCH.bit_length() - 1
    local_bits = stretch_count.bit_length() - 1
    ctx_bits = lax.axis_size("ctx").bit_length() - 1
    position = lax.axis_index("ctx")
    onehot = (level_index[:, None] == jnp.arange(plans, dtype=jnp.int32)[None, :]).astype(
        jnp.float32
    )
    token_weights = jnp.dot(
        onehot,
        level_table.reshape(plans, heads_here * level_total),
        precision=lax.Precision.HIGHEST,
        preferred_element_type=jnp.float32,
    )
    weight_blocks = token_weights.reshape(
        stretch_count, STRETCH, heads_here, level_total
    ).transpose(0, 2, 1, 3)
    query_blocks = queries.reshape(stretch_count, STRETCH, heads_here, head_size).transpose(
        0, 2, 1, 3
    )
    key_blocks = key_vectors.reshape(stretch_count, STRETCH, heads_here, head_size).transpose(
        0, 2, 1, 3
    )
    value_blocks = value_vectors.reshape(stretch_count, STRETCH, heads_here, head_size).transpose(
        0, 2, 1, 3
    )
    states = jnp.einsum(
        "nhsd,nhse->nhde", key_blocks, value_blocks, preferred_element_type=jnp.float32
    )
    own_total = jnp.sum(states, axis=0)
    zero_states = jnp.zeros((ctx_bits, heads_here, head_size, head_size), jnp.float32)
    shards = lax.all_gather(own_total[None].astype(jnp.bfloat16), "ctx", axis=0, tiled=True).astype(
        jnp.float32
    )
    sources = jnp.arange(shards.shape[0], dtype=jnp.int32)
    crossed = fenwick_level(jnp.bitwise_xor(position, sources), ctx_bits + 1)
    earlier = sources < position
    select = (
        (crossed[None, :] - 1 == jnp.arange(ctx_bits, dtype=jnp.int32)[:, None]) & earlier[None, :]
    ).astype(jnp.float32)
    remote = zero_states + jnp.einsum(
        "li,ihde->lhde", select, shards, precision=lax.Precision.HIGHEST
    )
    scores = jnp.einsum(
        "nhtd,nhsd->nhts", query_blocks, key_blocks, preferred_element_type=jnp.float32
    )
    offsets = jnp.arange(STRETCH, dtype=jnp.int32)
    levels = fenwick_level(jnp.bitwise_xor(offsets[:, None], offsets[None, :]), stretch_bits + 1)
    level_onehot = (
        levels[:, :, None] == jnp.arange(stretch_bits + 1, dtype=jnp.int32)[None, None, :]
    ).astype(jnp.float32)
    picked = jnp.einsum(
        "nhto,tso->nhts",
        weight_blocks[..., : stretch_bits + 1],
        level_onehot,
        precision=lax.Precision.HIGHEST,
    )
    causal = offsets[None, :] <= offsets[:, None]
    weighted = jnp.where(causal, scores * picked, 0.0).astype(jnp.bfloat16)
    output = jnp.einsum(
        "nhts,nhse->nhte", weighted, value_blocks, preferred_element_type=jnp.float32
    )
    level_list = []
    for bit_index in range(local_bits):
        span_width = 1 << bit_index
        groups = stretch_count // (2 * span_width)
        lower_sum = states.reshape(groups, 2, span_width, heads_here, head_size, head_size)[
            :, 0
        ].sum(axis=1)
        spread = jnp.broadcast_to(
            lower_sum[:, None], (groups, span_width, heads_here, head_size, head_size)
        )
        placed = jnp.stack([jnp.zeros_like(spread), spread], axis=1).reshape(
            stretch_count, heads_here, head_size, head_size
        )
        level_list.append(placed.astype(jnp.bfloat16))
    remote_rounded = remote.astype(jnp.bfloat16)
    for bit_index in range(ctx_bits):
        level_list.append(
            jnp.broadcast_to(
                remote_rounded[bit_index][None], (stretch_count, heads_here, head_size, head_size)
            )
        )
    all_levels = jnp.stack(level_list, axis=1)
    reached = jnp.einsum(
        "nhtd,nlhde->nhtle", query_blocks, all_levels, preferred_element_type=jnp.float32
    )
    level_scale = weight_blocks[..., stretch_bits + 1 : stretch_bits + 1 + local_bits + ctx_bits]
    output = output + jnp.sum(reached * level_scale[..., None], axis=3)
    normed = output * lax.rsqrt(jnp.mean(output * output, axis=-1, keepdims=True) + EPSILON)
    mixed_heads = (
        normed.astype(jnp.bfloat16).transpose(0, 2, 1, 3).reshape(tok_rows, heads_here * head_size)
    )
    return lax.psum_scatter(
        jnp.dot(mixed_heads, out_weight, preferred_element_type=jnp.float32).astype(jnp.bfloat16),
        "mp",
        scatter_dimension=0,
        tiled=True,
    )


def solution(mesh):
    placed = (
        P("ctx", "mp"),
        P("ctx", "mp"),
        P("ctx", "mp"),
        P("ctx"),
        P(None, "mp", None),
        P("mp", None),
    )
    return jax.shard_map(
        body, mesh=mesh, in_specs=placed, out_specs=P(("ctx", "mp"), None), check_vma=False
    )
```

profile of v0, /device:TPU:1, one launch (start us, length us, event | category | flops | bytes accessed | tf_op | source)
XLA Modules:
  0.0 208.8 jit_solution(399692076842779940)
XLA Ops:
  6.5 4.1 %reshape.194 = bf16[8,256,4,128]{3,2,1,0:T(4,128)(2,1)} reshape(bf16[2048,512]{1,0:T(8,128)(2,1)} %param.7) | data formatting | bytes 4194304 | tf_op jit(solution)/shard_map/reshape | solution.py:45
  10.6 4.2 %copy.55 = bf16[8,256,4,128]{1,3,2,0:T(8,128)(2,1)} copy(bf16[8,256,4,128]{3,2,1,0:T(4,128)(2,1)} %reshape.194) | data formatting | bytes 4194304 | tf_op jit(solution)/shard_map/transpose | solution.py:45
  14.8 4.0 %reshape.196 = bf16[8,256,4,128]{3,2,1,0:T(4,128)(2,1)} reshape(bf16[2048,512]{1,0:T(8,128)(2,1)} %param.8) | data formatting | bytes 4194304 | tf_op jit(solution)/shard_map/reshape | solution.py:48
  18.8 5.0 %fusion.68 = (bf16[4,128,128]{2,1,0:T(8,128)(2,1)}, bf16[8,4,128,128]{3,2,1,0:T(8,128)(2,1)S(1)}, f32[8,4,128,128]{3,2,1,0:T(8,128)}) fusion(bf16[8,256,4,128]{3,2,1,0:T(4,128)(2,1)} %reshape.196, bf16[8,256,4,128]{1,3,2,0:T(8,128)(2,1)} %copy.55), kind=kOutput, calls=%fused_computation.80 | convolution fusion | flops 269418496 | bytes 7471104 | tf_op jit(solution)/shard_map/nhsd,nhse->nhde/dot_general | solution.py:51
  26.1 2.1 slice_reduce_fusion.1
  30.2 2.0 copy.63
  32.5 2.4 %stack.15.clone = bf16[4,2,1,4,128,128]{4,5,3,1,0,2:T(8,128)(2,1)} pad(bf16[4,1,1,4,128,128]{4,5,3,1,0,2:T(8,128)(2,1)} %copy.63, bf16[]{:T(256)} %constant.7.clone.1), padding=0_0x1_0x0_0x0_0x0_0x0_0 | pad | bytes 1572866 | tf_op jit(solution)/shard_map/stack | solution.py:97
  36.3 4.0 %reshape.193 = bf16[8,256,4,128]{3,2,1,0:T(4,128)(2,1)} reshape(bf16[2048,512]{1,0:T(8,128)(2,1)} %param.6) | data formatting | bytes 4194304 | tf_op jit(solution)/shard_map/reshape | solution.py:42
  40.3 5.3 %copy.34 = f32[8,4,256,9]{3,0,1,2:T(8,128)} copy(f32[8,4,256,9]{2,3,1,0:T(8,128)} %slice.56) | data formatting | bytes 589824 | tf_op jit(solution)/shard_map/slice | solution.py:78
  46.4 2.9 %constant_dynamic-update-slice_fusion.2 = bf16[8,8,4,128,128]{3,4,1,2,0:T(8,128)(2,1)} fusion(bf16[8,1,4,128,128]{3,4,1,2,0:T(8,128)(2,1)} %bitcast.112), kind=kLoop, calls=%fused_computation.60 | loop fusion | bytes 2097152
  50.4 2.5 %constant_dynamic-update-slice_fusion = bf16[8,8,4,128,128]{3,4,1,2,0:T(8,128)(2,1)} fusion(bf16[8,8,4,128,128]{3,4,1,2,0:T(8,128)(2,1)} %constant_dynamic-update-slice_fusion.1, bf16[8,1,4,128,128]{3,4,1,2,0:T(8,128)(2,1)} %bitcast.113), kind=kLoop, calls=%fused_computation.58 | loop fusion | bytes 2097152
  52.9 6.5 %fusion.10 = f32[256,256,8,4]{1,2,3,0:T(8,128)} fusion(f32[8,4,256,9]{3,0,1,2:T(8,128)S(1)} %copy-done.1, s32[256,256]{1,0:T(8,128)S(1)} %convert_add_fusion), kind=kOutput, calls=%fused_computation.15 | convolution fusion | flops 227082240 | bytes 8945664 | tf_op jit(solution)/shard_map/nhto,tso->nhts/dot_general | solution.py:76
  59.4 14.3 %all-gather.3.cloned.1.call-done = bf16[128,128,128]{2,1,0:T(8,128)(2,1)} async-done(((bf16[4,128,128]{2,1,0:T(8,128)(2,1)}), bf16[128,128,128]{2,1,0:T(8,128)(2,1)}) %all-gather.3.cloned.1.call-update) | async-done | bytes 4194320 | tf_op jit(solution)/shard_map/all_gather | solution.py:56
  73.7 4.5 %fusion.39 = bf16[5,4,128,128]{3,0,2,1:T(8,128)(2,1)S(1)} fusion(bf16[32,4,128,128]{3,2,1,0:T(8,128)(2,1)} %bitcast.110, s32[32]{0:T(128)S(1)} %fusion.66, pred[32]{0:T(512)(128)(4,1)S(1)} %iota_compare_fusion.4), kind=kOutput, calls=%fused_computation.31 | convolution fusion | flops 21299520 | bytes 4849824 | tf_op jit(solution)/shard_map/li,ihde->lhde/dot_general | solution.py:65
  78.3 1.3 fusion.69
  80.3 1.2 broadcast_dynamic-update-slice_fusion.4
  83.9 1.2 broadcast_dynamic-update-slice_fusion.1
  85.1 1.2 broadcast_dynamic-update-slice_fusion
  86.3 9.3 %fusion = f32[8,4,256,128]{2,3,1,0:T(8,128)} fusion(f32[8,4,256,8]{2,3,1,0:T(8,128)S(1)} %copy-done.5, bf16[8,8,4,128,128]{3,4,1,2,0:T(8,128)(2,1)} %broadcast_dynamic-update-slice_fusion, bf16[8,256,4,128]{3,2,1,0:T(4,128)(2,1)S(1)} %copy-done.3), kind=kOutput, calls=%fused_computation.1 | convolution fusion | flops 2163212288 | bytes 14942208 | tf_op jit(solution)/shard_map/nhtd,nlhde->nhtle/dot_general | solution.py:109
  95.7 15.3 %multiply_reduce_fusion = (f32[8,4,256]{2,1,0:T(4,128)S(1)}, f32[8,4,256,128]{2,3,1,0:T(8,128)}) fusion(f32[8,4,256,128]{2,3,1,0:T(8,128)} %fusion, bf16[8,256,4,128]{3,2,1,0:T(4,128)(2,1)} %reshape.196, f32[256,256,8,4]{1,2,3,0:T(8,128)} %fusion.10, pred[256,256]{1,0:T(8,128)(4,1)S(1)} %copy-done.4, bf16[8,256,4,128]{1,3,2,0:T(8,128)(2,1)} %copy.55, ...), kind=kOutput, calls=%fused_computation.11 | convolution fusion | flops 1083170816 | bytes 23166976 | tf_op jit(solution)/shard_map/nhts,nhse->nhte/dot_general | solution.py:84
  111.0 2.7 %fusion.5 = bf16[8,256,4,128]{1,3,2,0:T(8,128)(2,1)S(1)} fusion(f32[8,4,256,128]{2,3,1,0:T(8,128)} %get-tuple-element.14, f32[8,256,4]{1,2,0:T(4,128)S(1)} %rsqrt_bitcast_fusion), kind=kLoop, calls=%fused_computation.8 | loop fusion | flops 2097152 | bytes 6324224 | tf_op jit(solution)/shard_map/convert_element_type | solution.py:116
  113.7 1.2 copy.47
  115.6 6.8 %convolution_convert_fusion = bf16[2048,2048]{1,0:T(8,128)(2,1)} fusion(bf16[2048,512]{0,1:T(8,128)(2,1)S(1)} %bitcast.115, bf16[512,2048]{1,0:T(8,128)(2,1)S(1)} %copy-done), kind=kOutput, calls=%fused_computation.5 | convolution fusion | flops 4299161600 | bytes 12582912 | tf_op jit(solution)/shard_map/dot_general | solution.py:119
  122.5 79.4 %reduce-scatter.2.cloned.1.call-done = bf16[512,2048]{1,0:T(8,128)(2,1)} async-done(((bf16[2048,2048]{1,0:T(8,128)(2,1)}), bf16[512,2048]{1,0:T(8,128)(2,1)}) %reduce-scatter.2.cloned.1.call-update) | async-done | bytes 2097168 | tf_op jit(solution)/shard_map/reduce_scatter | solution.py:118
  (48 shorter events, 11.7 us)
Async XLA Ops:
  6.5 109.1 %copy-start = (bf16[512,2048]{1,0:T(8,128)(2,1)S(1)}, bf16[512,2048]{1,0:T(8,128)(2,1)}, u32[]{:S(2)}) copy-start(bf16[512,2048]{1,0:T(8,128)(2,1)} %param.11) | copy-start | bytes 6291460
  6.5 67.2 %all-gather.3.cloned.1.call-start = ((), (), s32[]{:S(2)}) async-start(), calls=%async_computation.2 | async-start | bytes 4325376 | tf_op jit(solution)/shard_map/all_gather | solution.py:56
  18.8 5.0 %copy-start.6 = (f32[16,4,20]{2,1,0:T(4,128)S(1)}, f32[16,4,20]{2,1,0:T(4,128)}, u32[]{:S(2)}) copy-start(f32[16,4,20]{2,1,0:T(4,128)} %param.10) | copy-start | bytes 15364
  18.8 5.2 %copy-start.7 = (s32[2048]{0:T(1024)S(1)}, s32[2048]{0:T(1024)}, u32[]{:S(2)}) copy-start(s32[2048]{0:T(1024)} %param.9) | copy-start | bytes 24580
  23.8 178.1 %reduce-scatter.2.cloned.1.call-start = ((), (), s32[]{:S(2)}) async-start(), calls=%async_computation.1 | async-start | bytes 10485760 | tf_op jit(solution)/shard_map/reduce_scatter | solution.py:118
  32.2 2.6 %copy-start.2 = (f32[8,4,128,128]{3,2,1,0:T(8,128)S(1)}, f32[8,4,128,128]{3,2,1,0:T(8,128)}, u32[]{:S(2)}) copy-start(f32[8,4,128,128]{3,2,1,0:T(8,128)} %get-tuple-element.12) | copy-start | bytes 6291460
  45.6 7.3 %copy-start.1 = (f32[8,4,256,9]{3,0,1,2:T(8,128)S(1)}, f32[8,4,256,9]{3,0,1,2:T(8,128)}, u32[]{:S(2)}) copy-start(f32[8,4,256,9]{3,0,1,2:T(8,128)} %copy.34) | copy-start | bytes 884740
  80.3 6.0 %copy-start.3 = (bf16[8,256,4,128]{3,2,1,0:T(4,128)(2,1)S(1)}, bf16[8,256,4,128]{3,2,1,0:T(4,128)(2,1)}, u32[]{:S(2)}) copy-start(bf16[8,256,4,128]{3,2,1,0:T(4,128)(2,1)} %reshape.193) | copy-start | bytes 6291460
  80.3 6.0 %copy-start.5 = (f32[8,4,256,8]{2,3,1,0:T(8,128)S(1)}, f32[8,4,256,8]{2,3,1,0:T(8,128)}, u32[]{:S(2)}) copy-start(f32[8,4,256,8]{2,3,1,0:T(8,128)} %slice.65) | copy-start | bytes 786436
  86.3 9.3 %copy-start.4 = (pred[256,256]{1,0:T(8,128)(4,1)S(1)}, pred[256,256]{1,0:T(8,128)(4,1)}, u32[]{:S(2)}) copy-start(pred[256,256]{1,0:T(8,128)(4,1)} %iota_compare_fusion.1) | copy-start | bytes 196612
Sparse Core Ops, SparseCore 0:
  23.9 49.7 all-gather.2
  122.6 79.2 reduce-scatter.1
where the time goes:
time: 209 us
  waiting for transfers between devices  93.8 us (45%)
  matrix products  48 us (23%)
  local copies, waits for them, and re-layouts  47.7 us (23%)
  between operations  13.6 us (7%)
  other arithmetic  5.59 us (3%)
    reduce_scatter x1, waiting for transfers between devices, body(): lax.psum_scatter(jnp.dot(mixed_heads, out_weight, preferred_element_type=...  79.4 us
    dot_general x1, matrix products, body(): jnp.einsum('nhts,nhse->nhte', weighted, value_blocks, preferred_element_t...  15.3 us
    all_gather x1, waiting for transfers between devices, body(): lax.all_gather(own_total[None].astype(jnp.bfloat16), 'ctx', axis=0, tiled...  14.3 us
    unnamed x25, local copies, waits for them, and re-layouts  14 us
    dot_general x1, matrix products, body(): jnp.einsum('nhtd,nlhde->nhtle', query_blocks, all_levels, preferred_eleme...  9.34 us
    dot_general x1, matrix products, body(): jnp.dot(mixed_heads, out_weight, preferred_element_type=jnp.float32)  6.85 us
    dot_general x1, matrix products, body(): jnp.einsum('nhto,tso->nhts', weight_blocks[..., :stretch_bits + 1], level...  6.48 us
    slice x2, local copies, waits for them, and re-layouts, body(): weight_blocks[..., :stretch_bits + 1]  6.19 us
  transfers between devices with their start and end apart: 2, of which 2 were waited for; matrix products, arithmetic and copies ran while one was open for 17% of the time, Pallas kernels for 0%

commit v1 on v0

v1 whole, which is shorter than its diff:
```python
import functools

import jax
import jax.numpy as jnp
from jax import lax
from jax.experimental import pallas as pl
from jax.experimental.pallas import tpu as pltpu
from jax.sharding import PartitionSpec as P

EPSILON = 1e-06
BF = jnp.bfloat16
F32 = jnp.float32
MESH = pl.DeviceIdType.MESH

BLK = 256
HALF = 128
NBLK = 8
HEADS = 4
DH = 128
COLS = HEADS * DH
TOK = NBLK * BLK
RING = 4
OUT = 2048
OROWS = TOK // RING
LOCAL = 3
REMOTE = 5
LEVELS = 20
ZERO_LANE = 127


def dot(a, b):
    return jnp.dot(a, b, preferred_element_type=F32)


def dot_t(a, b):
    return lax.dot_general(a, b, (((1,), (1,)), ((), ())), preferred_element_type=F32)


def dot_tl(a, b):
    return lax.dot_general(a, b, (((0,), (0,)), ((), ())), preferred_element_type=F32)


def lanes(w, lane, rows):
    return jnp.broadcast_to(w[:, lane : lane + 1], (rows, DH))


def kernel(
    idx_ref, tab_ref, q_hbm, k_hbm, v_hbm, w_hbm, o_hbm,
    qv, kv, vv, wb, wt, pick, leaf, near, tot, tsend, trecv, zr, yr, far, acc, nb, rb, of, ob,
    kvsem, qsem, wsem, osem,
    t_s, t_r, z_s, z_r, y_s, y_r, l_s, l_r,
    wx_s, wx_r, wz_s, wz_r, wy_s, wy_r, wd_s, wd_r, a_s, a_r,
):
    ctx = lax.axis_index("ctx")
    x = lax.axis_index("mp")
    c = lax.rem(ctx, 2)
    z = lax.rem(ctx // 2, RING)
    y = ctx // (2 * RING)

    def place(yy, zz, cc):
        return (yy * RING + zz) * 2 + cc

    def plus(p, d):
        return lax.rem(p + d, RING)

    partner = {"ctx": place(y, z, 1 - c), "mp": x}

    def zpeer(p):
        return {"ctx": place(y, p, c), "mp": x}

    def ypeer(p):
        return {"ctx": place(p, z, c), "mp": x}

    def xpeer(p):
        return {"ctx": ctx, "mp": p}

    def rcopy(src, dst, s, r, dev):
        return pltpu.make_async_remote_copy(
            src_ref=src, dst_ref=dst, send_sem=s, recv_sem=r, device_id=dev, device_id_type=MESH
        )

    barrier = pltpu.get_barrier_semaphore()
    pl.semaphore_signal(barrier, inc=1, device_id=partner, device_id_type=MESH)
    for d in (1, 2, 3):
        for dev in (zpeer(plus(z, d)), ypeer(plus(y, d)), xpeer(plus(x, d))):
            pl.semaphore_signal(barrier, inc=1, device_id=dev, device_id_type=MESH)

    def rows(n, size=BLK):
        return pl.ds(pl.multiple_of(n * size, size), size)

    def kload(n):
        return pltpu.make_async_copy(k_hbm.at[rows(n)], kv.at[rows(n)], kvsem.at[0, n])

    def vload(n):
        return pltpu.make_async_copy(v_hbm.at[rows(n)], vv.at[rows(n)], kvsem.at[1, n])

    qload = pltpu.make_async_copy(q_hbm, qv, qsem)
    wload = pltpu.make_async_copy(w_hbm, wb.at[x], wsem)
    for n in range(NBLK):
        kload(n).start()
        vload(n).start()
    wload.start()
    qload.start()

    table = tab_ref[...]
    hi = table.astype(BF)
    rest = table - hi.astype(F32)
    mid = rest.astype(BF)
    low = (rest - mid.astype(F32)).astype(BF)
    table3 = jnp.concatenate([hi, mid, low], axis=0)
    plan = lax.broadcasted_iota(jnp.int32, (16, DH), 0)
    for i in range(TOK // DH):
        hot = (jnp.broadcast_to(idx_ref[i : i + 1, :], (16, DH)) == plan).astype(F32).astype(BF)
        wt[i * DH : (i + 1) * DH, :] = dot_tl(jnp.concatenate([hot, hot, hot], axis=0), table3)
    tt = lax.broadcasted_iota(jnp.int32, (HALF, HALF), 0)
    ss = lax.broadcasted_iota(jnp.int32, (HALF, HALF), 1)
    apart = jnp.bitwise_xor(tt, ss)
    level = jnp.zeros((HALF, HALF), jnp.int32)
    for bit in range(7):
        level = level + (apart >= (1 << bit)).astype(jnp.int32)
    for h in range(HEADS):
        pick[h] = jnp.where(ss <= tt, level + h * LEVELS, ZERO_LANE)

    def leaf_body(n, carry):
        kload(n).wait()
        vload(n).wait()
        for h in range(HEADS):
            col = slice(h * DH, (h + 1) * DH)
            leaf[n, h] = dot_tl(kv[rows(n), col], vv[rows(n), col])
        return carry

    lax.fori_loop(0, NBLK, leaf_body, 0)
    for h in range(HEADS):
        total = leaf[0, h]
        for n in range(1, NBLK):
            total = total + leaf[n, h]
        tot[h] = total
        tsend[h] = total.astype(BF)

    pl.semaphore_wait(barrier, 10)
    tcopy = rcopy(tsend, trecv, t_s, t_r, partner)
    tcopy.start()

    def piece_a(quarter, p):
        return wb.at[quarter, rows(p, DH), pl.ds(pl.multiple_of(c * 1024, 1024), 512)]

    def piece_b(quarter, p):
        return wb.at[quarter, rows(p, DH), pl.ds(pl.multiple_of(c * 1024 + 512, 512), 512)]

    def wx_a(quarter, d):
        return rcopy(piece_a(quarter, z), piece_a(quarter, z), wx_s.at[d - 1, 0], wx_r.at[quarter, 0], xpeer(plus(x, d)))

    def wx_b(quarter, d):
        return rcopy(piece_b(quarter, y), piece_b(quarter, y), wx_s.at[d - 1, 1], wx_r.at[quarter, 1], xpeer(plus(x, d)))

    wload.wait()
    for d in (1, 3, 2):
        wx_a(x, d).start()
        wx_b(x, d).start()

    zero = jnp.zeros((DH, DH), BF)

    def near_body(h, carry):
        l0, l2, l4, l6 = leaf[0, h], leaf[2, h], leaf[4, h], leaf[6, h]
        p0 = l0 + leaf[1, h]
        p4 = l4 + leaf[5, h]
        f0 = p0 + (l2 + leaf[3, h])
        first = [l0, l2, l4, l6]
        for n in range(NBLK):
            near[n, h, 0:DH, :] = first[n // 2].astype(BF) if n & 1 else zero
            near[n, h, DH : 2 * DH, :] = (p4 if n & 4 else p0).astype(BF) if n & 2 else zero
            near[n, h, 2 * DH : 3 * DH, :] = f0.astype(BF) if n & 4 else zero
        return carry

    lax.fori_loop(0, HEADS, near_body, 0)
    qload.wait()

    half0 = c * 2

    def zcopy(src, d):
        return rcopy(zr.at[src], zr.at[src], z_s.at[d - 1], z_r.at[src], zpeer(plus(z, d)))

    def ycopy(src, d):
        return rcopy(yr.at[src], yr.at[src], y_s.at[d - 1], y_r.at[src], ypeer(plus(y, d)))

    def choose(cond, value):
        return jnp.where(cond, value, jnp.zeros_like(value))

    def exchange_z():
        tcopy.wait_recv()
        for h in range(HEADS):
            got = trecv[h]
            far[h, 0:DH, :] = choose(c == 1, got.astype(F32)).astype(BF)
        for i in range(2):
            zr[z, i] = (tot[half0 + i] + trecv[half0 + i].astype(F32)).astype(BF)
        for d in (1, 3, 2):
            zcopy(z, d).start()

    def exchange_y():
        for d in (1, 2, 3):
            zcopy(plus(z, d), d).wait_recv()
        for i in range(2):
            parts = [zr[p, i].astype(F32) for p in range(RING)]
            lower = zr[jnp.maximum(z - 1, 0), i].astype(F32)
            pair = parts[0] + parts[1]
            far[half0 + i, DH : 2 * DH, :] = choose(lax.rem(z, 2) == 1, lower).astype(BF)
            far[half0 + i, 2 * DH : 3 * DH, :] = choose(z >= 2, pair).astype(BF)
            yr[y, i] = (pair + (parts[2] + parts[3])).astype(BF)
        for d in (1, 2, 3):

            @pl.when(y + d < RING)
            def _():
                ycopy(y, d).start()

    def lcopy():
        mine = far.at[pl.ds(half0, 2), pl.ds(DH, 4 * DH)]
        return rcopy(mine, mine, l_s, l_r, partner)

    def exchange_end():
        for d in (1, 2, 3):

            @pl.when(y >= d)
            def _():
                ycopy(y - d, d).wait_recv()

        for i in range(2):
            lower = yr[jnp.maximum(y - 1, 0), i].astype(F32)
            pair = yr[0, i].astype(F32) + yr[1, i].astype(F32)
            far[half0 + i, 3 * DH : 4 * DH, :] = choose(lax.rem(y, 2) == 1, lower).astype(BF)
            far[half0 + i, 4 * DH : 5 * DH, :] = choose(y >= 2, pair).astype(BF)
        lcopy().start()

    def near_attention(n, carry):
        r = rows(n)
        w = wt[r, :]
        for h in range(HEADS):
            col = slice(h * DH, (h + 1) * DH)
            q, k, v = qv[r, col], kv[r, col], vv[r, col]
            at = pick[h]
            s_lo = dot_t(q[:HALF], k[:HALF])
            s_hi = dot_t(q[HALF:], k)
            p_lo = (s_lo * jnp.take_along_axis(w[:HALF], at, axis=1, mode="promise_in_bounds")).astype(BF)
            p_hi = jnp.concatenate(
                [
                    (s_hi[:, :HALF] * lanes(w[HALF:], h * LEVELS + 8, HALF)).astype(BF),
                    (s_hi[:, HALF:] * jnp.take_along_axis(w[HALF:], at, axis=1, mode="promise_in_bounds")).astype(BF),
                ],
                axis=1,
            )
            qf = q.astype(F32)
            ql = jnp.concatenate(
                [(qf * lanes(w, h * LEVELS + 9 + j, BLK)).astype(BF) for j in range(LOCAL)], axis=1
            )
            o = jnp.concatenate([dot(p_lo, v[:HALF]), dot(p_hi, v)], axis=0)
            acc[r, col] = o + dot(ql, near[n, h])

        @pl.when(n == 0)
        def _():
            exchange_z()

        @pl.when(n == 4)
        def _():
            exchange_y()

        return carry

    lax.fori_loop(0, NBLK, near_attention, 0)
    exchange_end()

    def wz(quarter, src, d):
        return rcopy(piece_a(quarter, src), piece_a(quarter, src), wz_s.at[quarter, d - 1], wz_r.at[quarter, src], zpeer(plus(z, d)))

    def wy(quarter, src, d):
        return rcopy(piece_b(quarter, src), piece_b(quarter, src), wy_s.at[quarter, d - 1], wy_r.at[quarter, src], ypeer(plus(y, d)))

    sources = (3, 1, 2)
    for e in sources:
        quarter = plus(x, e)
        wx_a(quarter, 1).wait_recv()
        wx_b(quarter, 1).wait_recv()
        for d in (1, 3, 2):
            wz(quarter, z, d).start()
            wy(quarter, y, d).start()

    lcopy().wait_recv()

    def acopy(src, part, d):
        return rcopy(
            nb.at[rows(2 * plus(src, d) + part)],
            rb.at[src, pl.ds(part * BLK, BLK)],
            a_s.at[d - 1, part],
            a_r.at[src, part],
            xpeer(plus(src, d)),
        )

    def finish(n):
        r = rows(n)
        w = wt[r, :]
        for h in range(HEADS):
            col = slice(h * DH, (h + 1) * DH)
            qf = qv[r, col].astype(F32)
            ql = jnp.concatenate(
                [(qf * lanes(w, h * LEVELS + 12 + j, BLK)).astype(BF) for j in range(REMOTE)], axis=1
            )
            o = acc[r, col] + dot(ql, far[h])
            ms = jnp.mean(o * o, axis=-1, keepdims=True)
            nb[r, col] = (o * lax.rsqrt(ms + EPSILON)).astype(BF)

    order = (1, 3, 2, 0)

    def finish_body(j, carry):
        part = j // RING
        i = lax.rem(j, RING)
        d = jnp.where(i == 0, 1, jnp.where(i == 1, 3, jnp.where(i == 2, 2, 0)))
        finish(2 * plus(x, d) + part)
        for p in range(2):
            for m, dd in enumerate(order[:3]):

                @pl.when(j == p * RING + m)
                def _():
                    acopy(x, p, dd).start()

        return carry

    lax.fori_loop(0, 2 * RING, finish_body, 0)

    NC = 256

    def ocopy(part, i):
        return pltpu.make_async_copy(
            ob.at[pl.ds(part * BLK, BLK), rows(i, NC)], o_hbm.at[pl.ds(part * BLK, BLK), rows(i, NC)], osem.at[part, i]
        )

    def project(quarter, part, own, last):
        rws = slice(part * BLK, (part + 1) * BLK)

        def body(i, carry):
            cl = rows(i, NC)
            a = nb[rows(2 * x + part), :] if own else rb[quarter, rws, :]
            s = dot(a, wb[quarter, :, cl])
            if not own:
                s = s + of[rws, cl]
            if last:
                ob[rws, cl] = s.astype(BF)
                ocopy(part, i).start()
            else:
                of[rws, cl] = s
            return carry

        lax.fori_loop(0, OUT // NC, body, 0)

    for part in range(2):
        project(x, part, True, False)

    def half_of(quarter):
        return wb.at[quarter, :, pl.ds(pl.multiple_of(c * 1024, 1024), 1024)]

    def wd(quarter, e):
        return rcopy(half_of(quarter), half_of(quarter), wd_s.at[e - 1], wd_r.at[quarter], partner)

    for e in sources:
        quarter = plus(x, e)
        for d in (1, 2, 3):
            wz(quarter, plus(z, d), d).wait_recv()
            wy(quarter, plus(y, d), d).wait_recv()
        wd(quarter, e).start()

    for part in range(2):
        for e in sources:
            quarter = plus(x, e)
            if part == 0:
                wd(quarter, e).wait_recv()
            acopy(quarter, part, RING - e).wait_recv()
            project(quarter, part, False, e == sources[-1])

    tcopy.wait_send()
    lcopy().wait_send()
    for d in (1, 2, 3):
        zcopy(z, d).wait_send()

        @pl.when(y + d < RING)
        def _():
            ycopy(y, d).wait_send()

        wx_a(x, d).wait_send()
        wx_b(x, d).wait_send()
        quarter = plus(x, d)
        for dd in (1, 2, 3):
            wz(quarter, z, dd).wait_send()
            wy(quarter, y, dd).wait_send()
        wd(quarter, d).wait_send()
        for part in range(2):
            acopy(x, part, d).wait_send()
    for part in range(2):
        for i in range(OUT // NC):
            ocopy(part, i).wait()


def body(queries, key_vectors, value_vectors, level_index, level_table, out_weight):
    table = jnp.pad(level_table.reshape(16, HEADS * LEVELS), ((0, 0), (0, DH - HEADS * LEVELS)))
    index = level_index.reshape(TOK // DH, DH)
    anyspec = pl.BlockSpec(memory_space=pl.ANY)
    vspec = pl.BlockSpec(memory_space=pltpu.VMEM)
    dma = pltpu.SemaphoreType.DMA
    scratch = [
        pltpu.VMEM((TOK, COLS), BF),
        pltpu.VMEM((TOK, COLS), BF),
        pltpu.VMEM((TOK, COLS), BF),
        pltpu.VMEM((RING, COLS, OUT), BF),
        pltpu.VMEM((TOK, DH), F32),
        pltpu.VMEM((HEADS, HALF, HALF), jnp.int32),
        pltpu.VMEM((NBLK, HEADS, DH, DH), F32),
        pltpu.VMEM((NBLK, HEADS, LOCAL * DH, DH), BF),
        pltpu.VMEM((HEADS, DH, DH), F32),
        pltpu.VMEM((HEADS, DH, DH), BF),
        pltpu.VMEM((HEADS, DH, DH), BF),
        pltpu.VMEM((RING, 2, DH, DH), BF),
        pltpu.VMEM((RING, 2, DH, DH), BF),
        pltpu.VMEM((HEADS, REMOTE * DH, DH), BF),
        pltpu.VMEM((TOK, COLS), F32),
        pltpu.VMEM((TOK, COLS), BF),
        pltpu.VMEM((RING, OROWS, COLS), BF),
        pltpu.VMEM((OROWS, OUT), F32),
        pltpu.VMEM((OROWS, OUT), BF),
        dma((2, NBLK)), dma, dma, dma((2, 8)),
        dma, dma, dma((3,)), dma((RING,)), dma((3,)), dma((RING,)), dma, dma,
        dma((3, 2)), dma((RING, 2)), dma((RING, 3)), dma((RING, RING)), dma((RING, 3)), dma((RING, RING)),
        dma((3,)), dma((RING,)), dma((3, 2)), dma((RING, 2)),
    ]
    return pl.pallas_call(
        kernel,
        out_shape=jax.ShapeDtypeStruct((OROWS, OUT), BF),
        in_specs=[vspec, vspec, anyspec, anyspec, anyspec, anyspec],
        out_specs=anyspec,
        scratch_shapes=scratch,
        compiler_params=pltpu.CompilerParams(
            collective_id=0, has_side_effects=True, vmem_limit_bytes=60 * 1024 * 1024
        ),
    )(index, table, queries, key_vectors, value_vectors, out_weight)


def solution(mesh):
    placed = (
        P("ctx", "mp"),
        P("ctx", "mp"),
        P("ctx", "mp"),
        P("ctx"),
        P(None, "mp", None),
        P("mp", None),
    )
    return jax.shard_map(
        body, mesh=mesh, in_specs=placed, out_specs=P(("ctx", "mp"), None), check_vma=False
    )
```

time: 209 us -> 58.5 us (0.28)
  waiting for transfers between devices: 93.8 us -> 0 us
  Pallas kernels: 0 us -> 53.7 us
  matrix products: 48 us -> 0 us
  local copies, waits for them, and re-layouts: 47.7 us -> 4.6 us
  between operations: 13.6 us -> 0.01 us
  other arithmetic: 5.59 us -> 0 us
    reduce_scatter x1 -> x0, waiting for transfers between devices: 79.4 us -> none  [body(): lax.psum_scatter(jnp.dot(mixed_heads, out_weight, preferred_element_type=...]
    pallas_call x0 -> x1, Pallas kernels: none -> 53.7 us  [body(): pl.pallas_call(kernel, out_shape=jax.ShapeDtypeStruct((OROWS, OUT), BF),...]
    dot_general x7 -> x0, matrix products: 48 us -> none  [the longest x1 15.3 us: body(): jnp.einsum('nhts,nhse->nhte', weighted, value_blocks, preferred_element_t...]
    all_gather x1 -> x0, waiting for transfers between devices: 14.3 us -> none  [body(): lax.all_gather(own_total[None].astype(jnp.bfloat16), 'ctx', axis=0, tiled...]
    reshape x4 -> x1, local copies, waits for them, and re-layouts: 12.1 us -> 0.84 us  [body(): level_table.reshape(16, HEADS * LEVELS)]
    unnamed x25 -> x1, local copies, waits for them, and re-layouts: 14 us -> 3.16 us
    slice x10 -> x0, local copies, waits for them, and re-layouts: 9.82 us -> none  [the longest x2 6.19 us: body(): weight_blocks[..., :stretch_bits + 1]]
    another operation x8 -> x0, local copies, waits for them, and re-layouts: 6.31 us -> none  [the longest x5 3.85 us: body(): jnp.stack([jnp.zeros_like(spread), spread], axis=1)]
  transfers between devices with their start and end apart: 2 -> 0, of which waited for: 2 -> 0; matrix products, arithmetic and copies ran while one was open for 17% -> 0% of each run, Pallas kernels for 0% -> 0%
where the time goes in v1:
time: 58.5 us; the launch traced here: 58.3 us
  Pallas kernels  53.7 us (92%)
  local copies, waits for them, and re-layouts  4.6 us (8%)
    pallas_call x1, Pallas kernels, body(): pl.pallas_call(kernel, out_shape=jax.ShapeDtypeStruct((OROWS, OUT), BF),...  53.7 us
    unnamed x1, local copies, waits for them, and re-layouts  3.16 us

profile of v1, /device:TPU:1, one launch (start us, length us, event | category | flops | bytes accessed | tf_op | source)
XLA Modules:
  0.0 58.3 jit_solution(11225351063651539450)
XLA Ops:
  0.0 0.8 %reshape.7 = f32[16,80]{1,0:T(8,128)S(1)} reshape(f32[16,4,20]{2,1,0:T(4,128)} %param.10) | data formatting | bytes 10240 | tf_op jit(solution)/shard_map/reshape | solution.py:400
  0.8 0.6 %pad.4.tab_ref = f32[16,128]{1,0:T(8,128)} pad(f32[16,80]{1,0:T(8,128)S(1)} %reshape.7, f32[]{:T(128)} %constant.2.clone.1), padding=0_0x0_48 | pad | bytes 13316 | tf_op jit(solution)/shard_map/jit(_pad)/pad | solution.py:400
  1.4 53.7 %shard_map.64 = bf16[512,2048]{1,0:T(8,128)(2,1)} custom-call(s32[16,128]{1,0:T(8,128)} %bitcast.1, f32[16,128]{1,0:T(8,128)} %pad.4.tab_ref, bf16[2048,512]{1,0:T(8,128)(2,1)} %q_hbm.1, bf16[2048,512]{1,0:T(8,128)(2,1)} %k_hbm.1, bf16[2048,512]{1,0:T(8,128)(2,1)} %v_hbm.1, bf16[512,2048]{1,0:T(8,128)(2,1)} %w_hbm.1), custom_call_target="tpu_custom_call" | custom-call | tf_op jit(solution)/shard_map/pallas_call | solution.py:430
  55.1 3.2 %copy.8 = bf16[512,2048]{1,0:T(8,128)(2,1)} copy(bf16[512,2048]{1,0:T(8,128)(2,1)} %shard_map.64) | data formatting | bytes 4194304

commit v2 on v1

v2 whole, which is shorter than its diff:
```python
import functools

import jax
import jax.numpy as jnp
from jax import lax
from jax.experimental import pallas as pl
from jax.experimental.pallas import tpu as pltpu
from jax.sharding import PartitionSpec as P

EPSILON = 1e-06
BF = jnp.bfloat16
F32 = jnp.float32
MESH = pl.DeviceIdType.MESH

BLK = 256
HALF = 128
NBLK = 8
HEADS = 4
DH = 128
COLS = HEADS * DH
TOK = NBLK * BLK
RING = 4
OUT = 2048
OROWS = TOK // RING
LOCAL = 3
REMOTE = 5
LEVELS = 20
ZERO_LANE = 127


def dot(a, b):
    return jnp.dot(a, b, preferred_element_type=F32)


def dot_t(a, b):
    return lax.dot_general(a, b, (((1,), (1,)), ((), ())), preferred_element_type=F32)


def dot_tl(a, b):
    return lax.dot_general(a, b, (((0,), (0,)), ((), ())), preferred_element_type=F32)


def lanes(w, lane, rows):
    return jnp.broadcast_to(w[:, lane : lane + 1], (rows, DH))


def kernel(
    idx_ref, tab_ref, q_hbm, k_hbm, v_hbm, w_hbm, o_ref,
    qv, kv, vv, wb, wt, pick, leaf, near, tot, tsend, trecv, zr, yr, far, acc, ql_far, nb, rb,
    kvsem, qsem, wsem,
    t_s, t_r, z_s, z_r, y_s, y_r, l_s, l_r,
    wx_s, wx_r, wz_s, wz_r, wy_s, wy_r, wd_s, wd_r, a_s, a_r,
):
    ctx = lax.axis_index("ctx")
    x = lax.axis_index("mp")
    c = lax.rem(ctx, 2)
    z = lax.rem(ctx // 2, RING)
    y = ctx // (2 * RING)

    def place(yy, zz, cc):
        return (yy * RING + zz) * 2 + cc

    def plus(p, d):
        return lax.rem(p + d, RING)

    partner = {"ctx": place(y, z, 1 - c), "mp": x}

    def zpeer(p):
        return {"ctx": place(y, p, c), "mp": x}

    def ypeer(p):
        return {"ctx": place(p, z, c), "mp": x}

    def xpeer(p):
        return {"ctx": ctx, "mp": p}

    def rcopy(src, dst, s, r, dev):
        return pltpu.make_async_remote_copy(
            src_ref=src, dst_ref=dst, send_sem=s, recv_sem=r, device_id=dev, device_id_type=MESH
        )

    barrier = pltpu.get_barrier_semaphore()
    pl.semaphore_signal(barrier, inc=1, device_id=partner, device_id_type=MESH)
    for d in (1, 2, 3):
        for dev in (zpeer(plus(z, d)), ypeer(plus(y, d)), xpeer(plus(x, d))):
            pl.semaphore_signal(barrier, inc=1, device_id=dev, device_id_type=MESH)

    def rows(n, size=BLK):
        return pl.ds(pl.multiple_of(n * size, size), size)

    def kload(n):
        return pltpu.make_async_copy(k_hbm.at[rows(n)], kv.at[rows(n)], kvsem.at[0, n])

    def vload(n):
        return pltpu.make_async_copy(v_hbm.at[rows(n)], vv.at[rows(n)], kvsem.at[1, n])

    qload = pltpu.make_async_copy(q_hbm, qv, qsem)
    wload = pltpu.make_async_copy(w_hbm, wb.at[x], wsem)
    for n in range(NBLK):
        kload(n).start()
        vload(n).start()
    wload.start()
    qload.start()

    def leaf_body(n, carry):
        kload(n).wait()
        vload(n).wait()
        for h in range(HEADS):
            col = slice(h * DH, (h + 1) * DH)
            leaf[n, h] = dot_tl(kv[rows(n), col], vv[rows(n), col])
        return carry

    lax.fori_loop(0, NBLK, leaf_body, 0)
    for h in range(HEADS):
        total = leaf[0, h]
        for n in range(1, NBLK):
            total = total + leaf[n, h]
        tot[h] = total
        tsend[h] = total.astype(BF)

    pl.semaphore_wait(barrier, 10)
    tcopy = rcopy(tsend, trecv, t_s, t_r, partner)
    tcopy.start()

    def piece_a(quarter, p):
        return wb.at[quarter, rows(p, DH), pl.ds(pl.multiple_of(c * 1024, 1024), 512)]

    def piece_b(quarter, p):
        return wb.at[quarter, rows(p, DH), pl.ds(pl.multiple_of(c * 1024 + 512, 512), 512)]

    def wx_a(quarter, d):
        return rcopy(piece_a(quarter, z), piece_a(quarter, z), wx_s.at[d - 1, 0], wx_r.at[quarter, 0], xpeer(plus(x, d)))

    def wx_b(quarter, d):
        return rcopy(piece_b(quarter, y), piece_b(quarter, y), wx_s.at[d - 1, 1], wx_r.at[quarter, 1], xpeer(plus(x, d)))

    wload.wait()
    for d in (1, 3, 2):
        wx_a(x, d).start()
        wx_b(x, d).start()

    table = jnp.concatenate(
        [tab_ref[:, h, :] for h in range(HEADS)] + [jnp.zeros((16, DH - HEADS * LEVELS), F32)], axis=1
    )
    hi = table.astype(BF)
    rest = table - hi.astype(F32)
    mid = rest.astype(BF)
    low = (rest - mid.astype(F32)).astype(BF)
    table3 = jnp.concatenate([hi, mid, low], axis=0)
    plan = lax.broadcasted_iota(jnp.int32, (16, DH), 0)
    for i in range(TOK // DH):
        hot = (jnp.broadcast_to(idx_ref[i : i + 1, :], (16, DH)) == plan).astype(F32).astype(BF)
        wt[i * DH : (i + 1) * DH, :] = dot_tl(jnp.concatenate([hot, hot, hot], axis=0), table3)
    tt = lax.broadcasted_iota(jnp.int32, (HALF, HALF), 0)
    ss = lax.broadcasted_iota(jnp.int32, (HALF, HALF), 1)
    apart = jnp.bitwise_xor(tt, ss)
    level = jnp.zeros((HALF, HALF), jnp.int32)
    for bit in range(7):
        level = level + (apart >= (1 << bit)).astype(jnp.int32)
    for h in range(HEADS):
        pick[h] = jnp.where(ss <= tt, level + h * LEVELS, ZERO_LANE)

    zero = jnp.zeros((DH, DH), BF)

    def near_body(h, carry):
        l0, l2, l4, l6 = leaf[0, h], leaf[2, h], leaf[4, h], leaf[6, h]
        p0 = l0 + leaf[1, h]
        p4 = l4 + leaf[5, h]
        f0 = p0 + (l2 + leaf[3, h])
        first = [l0, l2, l4, l6]
        for n in range(NBLK):
            near[n, h, 0:DH, :] = first[n // 2].astype(BF) if n & 1 else zero
            near[n, h, DH : 2 * DH, :] = (p4 if n & 4 else p0).astype(BF) if n & 2 else zero
            near[n, h, 2 * DH : 3 * DH, :] = f0.astype(BF) if n & 4 else zero
        return carry

    lax.fori_loop(0, HEADS, near_body, 0)
    qload.wait()

    half0 = c * 2

    def zcopy(src, d, i):
        return rcopy(zr.at[src, i], zr.at[src, i], z_s.at[d - 1, i], z_r.at[src, i], zpeer(plus(z, d)))

    def ycopy(src, d, i):
        return rcopy(yr.at[src, i], yr.at[src, i], y_s.at[d - 1, i], y_r.at[src, i], ypeer(plus(y, d)))

    def lcopy(i):
        mine = far.at[half0 + i, pl.ds(DH, 4 * DH)]
        return rcopy(mine, mine, l_s.at[i], l_r.at[i], partner)

    def choose(cond, value):
        return jnp.where(cond, value, jnp.zeros_like(value))

    def exchange_z():
        tcopy.wait_recv()
        for i in range(2):
            zr[z, i] = (tot[half0 + i] + trecv[half0 + i].astype(F32)).astype(BF)
            for d in (2, 1, 3):
                zcopy(z, d, i).start()
        for h in range(HEADS):
            far[h, 0:DH, :] = choose(c == 1, trecv[h].astype(F32)).astype(BF)

    def exchange_y(i):
        for d in (1, 2, 3):
            zcopy(plus(z, d), d, i).wait_recv()
        parts = [zr[p, i].astype(F32) for p in range(RING)]
        pair = parts[0] + parts[1]
        yr[y, i] = (pair + (parts[2] + parts[3])).astype(BF)
        for d in (2, 1, 3):

            @pl.when(y + d < RING)
            def _():
                ycopy(y, d, i).start()

        lower = zr[jnp.maximum(z - 1, 0), i].astype(F32)
        far[half0 + i, DH : 2 * DH, :] = choose(lax.rem(z, 2) == 1, lower).astype(BF)
        far[half0 + i, 2 * DH : 3 * DH, :] = choose(z >= 2, pair).astype(BF)

    def exchange_end(i):
        for d in (1, 2, 3):

            @pl.when(y >= d)
            def _():
                ycopy(y - d, d, i).wait_recv()

        lower = yr[jnp.maximum(y - 1, 0), i].astype(F32)
        pair = yr[0, i].astype(F32) + yr[1, i].astype(F32)
        far[half0 + i, 3 * DH : 4 * DH, :] = choose(lax.rem(y, 2) == 1, lower).astype(BF)
        far[half0 + i, 4 * DH : 5 * DH, :] = choose(y >= 2, pair).astype(BF)
        lcopy(i).start()

    exchange_z()

    def near_attention(n, carry):
        r = rows(n)
        w = wt[r, :]
        for h in range(HEADS):
            col = slice(h * DH, (h + 1) * DH)
            q, k, v = qv[r, col], kv[r, col], vv[r, col]
            at = pick[h]
            s_lo = dot_t(q[:HALF], k[:HALF])
            s_hi = dot_t(q[HALF:], k)
            p_lo = (s_lo * jnp.take_along_axis(w[:HALF], at, axis=1, mode="promise_in_bounds")).astype(BF)
            p_hi = jnp.concatenate(
                [
                    (s_hi[:, :HALF] * lanes(w[HALF:], h * LEVELS + 8, HALF)).astype(BF),
                    (s_hi[:, HALF:] * jnp.take_along_axis(w[HALF:], at, axis=1, mode="promise_in_bounds")).astype(BF),
                ],
                axis=1,
            )
            qf = q.astype(F32)
            ql = jnp.concatenate(
                [(qf * lanes(w, h * LEVELS + 9 + j, BLK)).astype(BF) for j in range(LOCAL)], axis=1
            )
            o = jnp.concatenate([dot(p_lo, v[:HALF]), dot(p_hi, v)], axis=0)
            acc[r, col] = o + dot(ql, near[n, h])
            for j in range(REMOTE):
                ql_far[r, (h * REMOTE + j) * DH : (h * REMOTE + j + 1) * DH] = (
                    qf * lanes(w, h * LEVELS + 12 + j, BLK)
                ).astype(BF)

        for at_n, hook in hooks:

            @pl.when(n == at_n)
            def _():
                hook()

        return carry

    def wz(quarter, src, d):
        return rcopy(piece_a(quarter, src), piece_a(quarter, src), wz_s.at[quarter, d - 1], wz_r.at[quarter, src], zpeer(plus(z, d)))

    def wy(quarter, src, d):
        return rcopy(piece_b(quarter, src), piece_b(quarter, src), wy_s.at[quarter, d - 1], wy_r.at[quarter, src], ypeer(plus(y, d)))

    sources = (3, 1, 2)

    def send_wz(es):
        for e in es:
            wx_a(plus(x, e), 1).wait_recv()
            for d in (2, 1, 3):
                wz(plus(x, e), z, d).start()

    hooks = (
        (3, lambda: exchange_y(0)),
        (4, lambda: exchange_y(1)),
        (6, lambda: send_wz((3, 1))),
        (7, lambda: exchange_end(0)),
    )
    lax.fori_loop(0, NBLK, near_attention, 0)
    exchange_end(1)
    send_wz((2,))
    for e in sources:
        wx_b(plus(x, e), 1).wait_recv()
        for d in (2, 1, 3):
            wy(plus(x, e), y, d).start()

    def acopy(src, slot, d):
        own = lax.rem(slot + c, 2)
        block = 2 * plus(src, d)
        if slot < 2:
            cols = pl.ds(pl.multiple_of(own * 2 * DH, 2 * DH), 2 * DH)
            here = nb.at[rows(block), cols]
            there = rb.at[src, pl.ds(0, BLK), cols]
        else:
            here = nb.at[rows(2 * block + slot, HALF)]
            there = rb.at[src, pl.ds(slot * HALF, HALF)]
        return rcopy(here, there, a_s.at[d - 1, slot], a_r.at[src, slot], xpeer(plus(src, d)))

    def finish(n, pair):
        r = rows(n)
        for i in range(2):
            h = 2 * pair + i
            col = pl.ds(pl.multiple_of(h * DH, DH), DH)
            wide = pl.ds(pl.multiple_of(h * REMOTE * DH, DH), REMOTE * DH)
            o = acc[r, col] + dot(ql_far[r, wide], far[h])
            ms = jnp.mean(o * o, axis=-1, keepdims=True)
            nb[r, col] = (o * lax.rsqrt(ms + EPSILON)).astype(BF)

    order = (2, 1, 3)

    def offset(i):
        return jnp.where(i == 0, order[0], jnp.where(i == 1, order[1], jnp.where(i == 2, order[2], 0)))

    def send_slots(i, slots):
        for m, d in enumerate(order):

            @pl.when(i == m)
            def _():
                for slot in slots:
                    acopy(x, slot, d).start()

    def early(slot):
        def body(i, carry):
            finish(2 * plus(x, offset(i)), lax.rem(slot + c, 2))
            send_slots(i, (slot,))
            return carry

        lax.fori_loop(0, 3, body, 0)

    def late(i, carry):
        n = 2 * plus(x, offset(i)) + 1
        finish(n, 0)
        finish(n, 1)
        send_slots(i, (2, 3))
        return carry

    early(0)
    for i in range(2):
        theirs = far.at[2 * (1 - c) + i, pl.ds(DH, 4 * DH)]
        rcopy(theirs, theirs, l_s.at[i], l_r.at[i], partner).wait_recv()
    early(1)
    lax.fori_loop(0, 4, late, 0)
    finish(2 * x, 0)
    finish(2 * x, 1)

    NC = 512

    def project(row, size):
        rws = pl.ds(row, size)

        def body(i, carry):
            cl = rows(i, NC)
            s = dot(nb[pl.ds(pl.multiple_of(x * OROWS, OROWS) + row, size), :], wb[x, :, cl])
            for e in sources:
                s = s + dot(rb[plus(x, e), rws, :], wb[plus(x, e), :, cl])
            o_ref[rws, cl] = s.astype(BF)
            return carry

        lax.fori_loop(0, OUT // NC, body, 0)

    def half_of(quarter):
        return wb.at[quarter, :, pl.ds(pl.multiple_of(c * 1024, 1024), 1024)]

    def wd(quarter, e):
        return rcopy(half_of(quarter), half_of(quarter), wd_s.at[e - 1], wd_r.at[quarter], partner)

    for e in sources:
        quarter = plus(x, e)
        for d in (1, 2, 3):
            wz(quarter, plus(z, d), d).wait_recv()
            wy(quarter, plus(y, d), d).wait_recv()
        wd(quarter, e).start()

    for e in sources:
        wd(plus(x, e), e).wait_recv()
    for slot in range(4):
        for e in sources:
            acopy(plus(x, e), slot, RING - e).wait_recv()
        if slot == 1:
            project(0, BLK)
        elif slot > 1:
            project(slot * HALF, HALF)

    tcopy.wait_send()
    for i in range(2):
        lcopy(i).wait_send()
    for d in (1, 2, 3):
        for i in range(2):
            zcopy(z, d, i).wait_send()

            @pl.when(y + d < RING)
            def _():
                ycopy(y, d, i).wait_send()

        wx_a(x, d).wait_send()
        wx_b(x, d).wait_send()
        quarter = plus(x, d)
        for dd in (1, 2, 3):
            wz(quarter, z, dd).wait_send()
            wy(quarter, y, dd).wait_send()
        wd(quarter, d).wait_send()
        for slot in range(4):
            acopy(x, slot, d).wait_send()


def body(queries, key_vectors, value_vectors, level_index, level_table, out_weight):
    index = level_index.reshape(TOK // DH, DH)
    anyspec = pl.BlockSpec(memory_space=pl.ANY)
    vspec = pl.BlockSpec(memory_space=pltpu.VMEM)
    dma = pltpu.SemaphoreType.DMA
    scratch = [
        pltpu.VMEM((TOK, COLS), BF),
        pltpu.VMEM((TOK, COLS), BF),
        pltpu.VMEM((TOK, COLS), BF),
        pltpu.VMEM((RING, COLS, OUT), BF),
        pltpu.VMEM((TOK, DH), F32),
        pltpu.VMEM((HEADS, HALF, HALF), jnp.int32),
        pltpu.VMEM((NBLK, HEADS, DH, DH), F32),
        pltpu.VMEM((NBLK, HEADS, LOCAL * DH, DH), BF),
        pltpu.VMEM((HEADS, DH, DH), F32),
        pltpu.VMEM((HEADS, DH, DH), BF),
        pltpu.VMEM((HEADS, DH, DH), BF),
        pltpu.VMEM((RING, 2, DH, DH), BF),
        pltpu.VMEM((RING, 2, DH, DH), BF),
        pltpu.VMEM((HEADS, REMOTE * DH, DH), BF),
        pltpu.VMEM((TOK, COLS), F32),
        pltpu.VMEM((TOK, HEADS * REMOTE * DH), BF),
        pltpu.VMEM((TOK, COLS), BF),
        pltpu.VMEM((RING, OROWS, COLS), BF),
        dma((2, NBLK)), dma, dma,
        dma, dma, dma((3, 2)), dma((RING, 2)), dma((3, 2)), dma((RING, 2)), dma((2,)), dma((2,)),
        dma((3, 2)), dma((RING, 2)), dma((RING, 3)), dma((RING, RING)), dma((RING, 3)), dma((RING, RING)),
        dma((3,)), dma((RING,)), dma((3, 4)), dma((RING, 4)),
    ]
    return pl.pallas_call(
        kernel,
        out_shape=pltpu.VMEM((OROWS, OUT), BF),
        in_specs=[vspec, vspec, anyspec, anyspec, anyspec, anyspec],
        out_specs=vspec,
        scratch_shapes=scratch,
        compiler_params=pltpu.CompilerParams(
            collective_id=0, has_side_effects=True, vmem_limit_bytes=56 * 1024 * 1024
        ),
    )(index, level_table, queries, key_vectors, value_vectors, out_weight)


def solution(mesh):
    placed = (
        P("ctx", "mp"),
        P("ctx", "mp"),
        P("ctx", "mp"),
        P("ctx"),
        P(None, "mp", None),
        P("mp", None),
    )
    return jax.shard_map(
        body, mesh=mesh, in_specs=placed, out_specs=P(("ctx", "mp"), None), check_vma=False
    )
```

time: 58.5 us -> 54.2 us (0.926)
  local copies, waits for them, and re-layouts: 4.6 us -> 1.32 us
  Pallas kernels: 53.7 us -> 52.7 us
    unnamed x1, local copies, waits for them, and re-layouts: 3.16 us -> 1.32 us
    pallas_call x1, Pallas kernels: 53.7 us -> 52.7 us  [body(): pl.pallas_call(kernel, out_shape=pltpu.VMEM((OROWS, OUT), BF), in_specs=[...]
    reshape x1 -> x0, local copies, waits for them, and re-layouts: 0.84 us -> none  [body(): level_table.reshape(16, HEADS * LEVELS)]
    pad x1 -> x0, local copies, waits for them, and re-layouts: 0.61 us -> none  [body(): jnp.pad(level_table.reshape(16, HEADS * LEVELS), ((0, 0), (0, DH - HEADS...]
where the time goes in v2:
time: 54.2 us; the launch traced here: 54.1 us
  Pallas kernels  52.7 us (97%)
  local copies, waits for them, and re-layouts  1.32 us (2%)
    pallas_call x1, Pallas kernels, body(): pl.pallas_call(kernel, out_shape=pltpu.VMEM((OROWS, OUT), BF), in_specs=[...  52.7 us
    unnamed x1, local copies, waits for them, and re-layouts  1.32 us

profile of v2, /device:TPU:1, one launch (start us, length us, event | category | flops | bytes accessed | tf_op | source)
XLA Modules:
  0.0 54.1 jit_solution(9740111853500347686)
XLA Ops:
  0.0 52.7 %shard_map.64 = bf16[512,2048]{1,0:T(8,128)(2,1)S(1)} custom-call(s32[16,128]{1,0:T(8,128)} %bitcast.1, f32[16,4,20]{2,1,0:T(4,128)} %tab_ref.1, bf16[2048,512]{1,0:T(8,128)(2,1)} %q_hbm.1, bf16[2048,512]{1,0:T(8,128)(2,1)} %k_hbm.1, bf16[2048,512]{1,0:T(8,128)(2,1)} %v_hbm.1, bf16[512,2048]{1,0:T(8,128)(2,1)} %w_hbm.1), custom_call_target="tpu_custom_call" | custom-call | tf_op jit(solution)/shard_map/pallas_call | solution.py:447
  52.7 1.3 %copy.8 = bf16[512,2048]{1,0:T(8,128)(2,1)} copy(bf16[512,2048]{1,0:T(8,128)(2,1)S(1)} %shard_map.64) | data formatting | bytes 4194304

commit v3 on v2

--- a/solution.py
+++ b/solution.py
@@ -40,6 +40,27 @@
     return lax.dot_general(a, b, (((0,), (0,)), ((), ())), preferred_element_type=F32)
 
 
+GATHER = lax.GatherDimensionNumbers(
+    offset_dims=(),
+    collapsed_slice_dims=(1,),
+    start_index_map=(1,),
+    operand_batching_dims=(0,),
+    start_indices_batching_dims=(0,),
+)
+
+
+def pick_lanes(w, at):
+    return lax.gather(w, at[..., None], GATHER, (1, 1), mode=lax.GatherScatterMode.PROMISE_IN_BOUNDS)
+
+
+def beside(*parts):
+    return jnp.concatenate(parts, axis=1)
+
+
+def stacked(*parts):
+    return jnp.concatenate(parts, axis=0)
+
+
 def lanes(w, lane, rows):
     return jnp.broadcast_to(w[:, lane : lane + 1], (rows, DH))
 
@@ -99,12 +120,16 @@
     for n in range(NBLK):
         kload(n).start()
         vload(n).start()
-    wload.start()
-    qload.start()
 
     def leaf_body(n, carry):
         kload(n).wait()
         vload(n).wait()
+
+        @pl.when(n == 3)
+        def _():
+            wload.start()
+            qload.start()
+
         for h in range(HEADS):
             col = slice(h * DH, (h + 1) * DH)
             leaf[n, h] = dot_tl(kv[rows(n), col], vv[rows(n), col])
@@ -162,22 +187,23 @@
 
     zero = jnp.zeros((DH, DH), BF)
 
-    def near_body(h, carry):
+    for h in range(HEADS):
         l0, l2, l4, l6 = leaf[0, h], leaf[2, h], leaf[4, h], leaf[6, h]
         p0 = l0 + leaf[1, h]
         p4 = l4 + leaf[5, h]
         f0 = p0 + (l2 + leaf[3, h])
-        first = [l0, l2, l4, l6]
-        for n in range(NBLK):
-            near[n, h, 0:DH, :] = first[n // 2].astype(BF) if n & 1 else zero
-            near[n, h, DH : 2 * DH, :] = (p4 if n & 4 else p0).astype(BF) if n & 2 else zero
-            near[n, h, 2 * DH : 3 * DH, :] = f0.astype(BF) if n & 4 else zero
-        return carry
-
-    lax.fori_loop(0, HEADS, near_body, 0)
+        near[h, 0] = zero
+        for i, node in enumerate((l0, l2, l4, l6, p0, p4, f0)):
+            near[h, 1 + i] = node.astype(BF)
+    for p in range(2):
+        far[p, 0 : REMOTE * DH, DH:] = jnp.zeros((REMOTE * DH, DH), BF)
+        far[p, REMOTE * DH :, :DH] = jnp.zeros((REMOTE * DH, DH), BF)
     qload.wait()
 
     half0 = c * 2
+
+    def far_at(pair, i, first, count):
+        return far.at[pair, pl.ds((i * REMOTE + first) * DH, count * DH), pl.ds(i * DH, DH)]
 
     def zcopy(src, d, i):
         return rcopy(zr.at[src, i], zr.at[src, i], z_s.at[d - 1, i], z_r.at[src, i], zpeer(plus(z, d)))
@@ -186,7 +212,7 @@
         return rcopy(yr.at[src, i], yr.at[src, i], y_s.at[d - 1, i], y_r.at[src, i], ypeer(plus(y, d)))
 
     def lcopy(i):
-        mine = far.at[half0 + i, pl.ds(DH, 4 * DH)]
+        mine = far_at(c, i, 1, 4)
         return rcopy(mine, mine, l_s.at[i], l_r.at[i], partner)
 
     def choose(cond, value):
@@ -199,7 +225,7 @@
             for d in (2, 1, 3):
                 zcopy(z, d, i).start()
         for h in range(HEADS):
-            far[h, 0:DH, :] = choose(c == 1, trecv[h].astype(F32)).astype(BF)
+            far_at(h // 2, h % 2, 0, 1)[...] = choose(c == 1, trecv[h].astype(F32)).astype(BF)
 
     def exchange_y(i):
         for d in (1, 2, 3):
@@ -214,8 +240,8 @@
                 ycopy(y, d, i).start()
 
         lower = zr[jnp.maximum(z - 1, 0), i].astype(F32)
-        far[half0 + i, DH : 2 * DH, :] = choose(lax.rem(z, 2) == 1, lower).astype(BF)
-        far[half0 + i, 2 * DH : 3 * DH, :] = choose(z >= 2, pair).astype(BF)
+        far_at(c, i, 1, 1)[...] = choose(lax.rem(z, 2) == 1, lower).astype(BF)
+        far_at(c, i, 2, 1)[...] = choose(z >= 2, pair).astype(BF)
 
     def exchange_end(i):
         for d in (1, 2, 3):
@@ -226,8 +252,8 @@
 
         lower = yr[jnp.maximum(y - 1, 0), i].astype(F32)
         pair = yr[0, i].astype(F32) + yr[1, i].astype(F32)
-        far[half0 + i, 3 * DH : 4 * DH, :] = choose(lax.rem(y, 2) == 1, lower).astype(BF)
-        far[half0 + i, 4 * DH : 5 * DH, :] = choose(y >= 2, pair).astype(BF)
+        far_at(c, i, 3, 1)[...] = choose(lax.rem(y, 2) == 1, lower).astype(BF)
+        far_at(c, i, 4, 1)[...] = choose(y >= 2, pair).astype(BF)
         lcopy(i).start()
 
     exchange_z()
@@ -235,30 +261,46 @@
     def near_attention(n, carry):
         r = rows(n)
         w = wt[r, :]
-        for h in range(HEADS):
-            col = slice(h * DH, (h + 1) * DH)
-            q, k, v = qv[r, col], kv[r, col], vv[r, col]
-            at = pick[h]
-            s_lo = dot_t(q[:HALF], k[:HALF])
-            s_hi = dot_t(q[HALF:], k)
-            p_lo = (s_lo * jnp.take_along_axis(w[:HALF], at, axis=1, mode="promise_in_bounds")).astype(BF)
-            p_hi = jnp.concatenate(
-                [
-                    (s_hi[:, :HALF] * lanes(w[HALF:], h * LEVELS + 8, HALF)).astype(BF),
-                    (s_hi[:, HALF:] * jnp.take_along_axis(w[HALF:], at, axis=1, mode="promise_in_bounds")).astype(BF),
-                ],
-                axis=1,
+        w16 = w.astype(BF)
+        which = (
+            jnp.where(lax.rem(n, 2) == 1, 1 + n // 2, 0),
+            jnp.where(lax.rem(n // 2, 2) == 1, jnp.where(n >= 4, 6, 5), 0),
+            jnp.where(n >= 4, 7, 0),
+        )
+        z_lo, z_hi = jnp.zeros((HALF, DH), BF), jnp.zeros((BLK, DH), BF)
+        for p in range(2):
+            low, high, near_q, values = [], [], [], []
+            for h in (2 * p, 2 * p + 1):
+                col = slice(h * DH, (h + 1) * DH)
+                q, k, v = qv[r, col], kv[r, col], vv[r, col]
+                at = pick[h]
+                s_lo = dot_t(q[:HALF], k[:HALF])
+                s_hi = dot_t(q[HALF:], k)
+                low.append((s_lo * pick_lanes(w[:HALF], at)).astype(BF))
+                high.append((s_hi[:, :HALF] * lanes(w16[HALF:], h * LEVELS + 8, HALF).astype(F32)).astype(BF))
+                high.append((s_hi[:, HALF:] * pick_lanes(w[HALF:], at)).astype(BF))
+                for j in range(LOCAL):
+                    near_q.append(q * lanes(w16, h * LEVELS + 9 + j, BLK))
+                for j in range(REMOTE):
+                    ql_far[r, (h * REMOTE + j) * DH : (h * REMOTE + j + 1) * DH] = q * lanes(
+                        w16, h * LEVELS + 12 + j, BLK
+                    )
+                values.append(v)
+            va, vb = values
+            nodes_a, nodes_b = ([near[h, t] for t in which] for h in (2 * p, 2 * p + 1))
+            states = stacked(
+                *[beside(t, zero) for t in nodes_a],
+                *[beside(zero, t) for t in nodes_b],
             )
-            qf = q.astype(F32)
-            ql = jnp.concatenate(
-                [(qf * lanes(w, h * LEVELS + 9 + j, BLK)).astype(BF) for j in range(LOCAL)], axis=1
+            pair = slice(2 * p * DH, 2 * (p + 1) * DH)
+            acc[rows(2 * n, HALF), pair] = dot(
+                beside(*low, *[t[:HALF] for t in near_q]),
+                stacked(beside(va[:HALF], z_lo), beside(z_lo, vb[:HALF]), states),
             )
-            o = jnp.concatenate([dot(p_lo, v[:HALF]), dot(p_hi, v)], axis=0)
-            acc[r, col] = o + dot(ql, near[n, h])
-            for j in range(REMOTE):
-                ql_far[r, (h * REMOTE + j) * DH : (h * REMOTE + j + 1) * DH] = (
-                    qf * lanes(w, h * LEVELS + 12 + j, BLK)
-                ).astype(BF)
+            acc[rows(2 * n + 1, HALF), pair] = dot(
+                beside(*high, *[t[HALF:] for t in near_q]),
+                stacked(beside(va, z_hi), beside(z_hi, vb), states),
+            )
 
         for at_n, hook in hooks:
 
@@ -283,12 +325,12 @@
                 wz(plus(x, e), z, d).start()
 
     hooks = (
-        (3, lambda: exchange_y(0)),
-        (4, lambda: exchange_y(1)),
-        (6, lambda: send_wz((3, 1))),
-        (7, lambda: exchange_end(0)),
+        (5, lambda: exchange_y(0)),
+        (7, lambda: exchange_y(1)),
     )
     lax.fori_loop(0, NBLK, near_attention, 0)
+    send_wz((3, 1))
+    exchange_end(0)
     exchange_end(1)
     send_wz((2,))
     for e in sources:
@@ -310,13 +352,14 @@
 
     def finish(n, pair):
         r = rows(n)
-        for i in range(2):
-            h = 2 * pair + i
-            col = pl.ds(pl.multiple_of(h * DH, DH), DH)
-            wide = pl.ds(pl.multiple_of(h * REMOTE * DH, DH), REMOTE * DH)
-            o = acc[r, col] + dot(ql_far[r, wide], far[h])
-            ms = jnp.mean(o * o, axis=-1, keepdims=True)
-            nb[r, col] = (o * lax.rsqrt(ms + EPSILON)).astype(BF)
+        col = pl.ds(pl.multiple_of(pair * 2 * DH, 2 * DH), 2 * DH)
+        wide = pl.ds(pl.multiple_of(pair * 2 * REMOTE * DH, 2 * REMOTE * DH), 2 * REMOTE * DH)
+        o = acc[r, col] + dot(ql_far[r, wide], far[pair])
+        done = []
+        for t in (o[:, :DH], o[:, DH:]):
+            ms = jnp.mean(t * t, axis=-1, keepdims=True)
+            done.append((t * lax.rsqrt(ms + EPSILON)).astype(BF))
+        nb[r, col] = beside(*done)
 
     order = (2, 1, 3)
 
@@ -348,7 +391,7 @@
 
     early(0)
     for i in range(2):
-        theirs = far.at[2 * (1 - c) + i, pl.ds(DH, 4 * DH)]
+        theirs = far_at(1 - c, i, 1, 4)
         rcopy(theirs, theirs, l_s.at[i], l_r.at[i], partner).wait_recv()
     early(1)
     lax.fori_loop(0, 4, late, 0)
@@ -428,13 +471,13 @@
         pltpu.VMEM((TOK, DH), F32),
         pltpu.VMEM((HEADS, HALF, HALF), jnp.int32),
         pltpu.VMEM((NBLK, HEADS, DH, DH), F32),
-        pltpu.VMEM((NBLK, HEADS, LOCAL * DH, DH), BF),
+        pltpu.VMEM((HEADS, 8, DH, DH), BF),
         pltpu.VMEM((HEADS, DH, DH), F32),
         pltpu.VMEM((HEADS, DH, DH), BF),
         pltpu.VMEM((HEADS, DH, DH), BF),
         pltpu.VMEM((RING, 2, DH, DH), BF),
         pltpu.VMEM((RING, 2, DH, DH), BF),
-        pltpu.VMEM((HEADS, REMOTE * DH, DH), BF),
+        pltpu.VMEM((2, 2 * REMOTE * DH, 2 * DH), BF),
         pltpu.VMEM((TOK, COLS), F32),
         pltpu.VMEM((TOK, HEADS * REMOTE * DH), BF),
         pltpu.VMEM((TOK, COLS), BF),

time: 54.2 us -> 52.4 us (0.967)
  Pallas kernels: 52.7 us -> 50.9 us
    pallas_call x1, Pallas kernels: 52.7 us -> 50.9 us  [body(): pl.pallas_call(kernel, out_shape=pltpu.VMEM((OROWS, OUT), BF), in_specs=[...]
where the time goes in v3:
time: 52.4 us; the launch traced here: 52.2 us
  Pallas kernels  50.9 us (97%)
  local copies, waits for them, and re-layouts  1.32 us (3%)
    pallas_call x1, Pallas kernels, body(): pl.pallas_call(kernel, out_shape=pltpu.VMEM((OROWS, OUT), BF), in_specs=[...  50.9 us
    unnamed x1, local copies, waits for them, and re-layouts  1.32 us

profile of v3, /device:TPU:1, one launch (start us, length us, event | category | flops | bytes accessed | tf_op | source)
XLA Modules:
  0.0 52.2 jit_solution(16451093087047170766)
XLA Ops:
  0.0 50.9 %shard_map.64 = bf16[512,2048]{1,0:T(8,128)(2,1)S(1)} custom-call(s32[16,128]{1,0:T(8,128)} %bitcast.1, f32[16,4,20]{2,1,0:T(4,128)} %tab_ref.1, bf16[2048,512]{1,0:T(8,128)(2,1)} %q_hbm.1, bf16[2048,512]{1,0:T(8,128)(2,1)} %k_hbm.1, bf16[2048,512]{1,0:T(8,128)(2,1)} %v_hbm.1, bf16[512,2048]{1,0:T(8,128)(2,1)} %w_hbm.1), custom_call_target="tpu_custom_call" | custom-call | tf_op jit(solution)/shard_map/pallas_call | solution.py:490
  50.9 1.3 %copy.8 = bf16[512,2048]{1,0:T(8,128)(2,1)} copy(bf16[512,2048]{1,0:T(8,128)(2,1)S(1)} %shard_map.64) | data formatting | bytes 4194304

commit v4 on v3

--- a/solution.py
+++ b/solution.py
@@ -67,10 +67,10 @@
 
 def kernel(
     idx_ref, tab_ref, q_hbm, k_hbm, v_hbm, w_hbm, o_ref,
-    qv, kv, vv, wb, wt, pick, leaf, near, tot, tsend, trecv, zr, yr, far, acc, ql_far, nb, rb,
+    qv, kv, vv, wb, wt, pick, leaf, near, tot, tsend, trecv, zr, yr, far, acc, ql_far, nb, rb, own,
     kvsem, qsem, wsem,
     t_s, t_r, z_s, z_r, y_s, y_r, l_s, l_r,
-    wx_s, wx_r, wz_s, wz_r, wy_s, wy_r, wd_s, wd_r, a_s, a_r,
+    wx_s, wx_r, wz_s, wz_r, wy_s, wy_r, fz_s, fz_r, fy_s, fy_r, wd_s, wd_r, a_s, a_r,
 ):
     ctx = lax.axis_index("ctx")
     x = lax.axis_index("mp")
@@ -120,15 +120,13 @@
     for n in range(NBLK):
         kload(n).start()
         vload(n).start()
+        if n == 3:
+            wload.start()
+    qload.start()
 
     def leaf_body(n, carry):
         kload(n).wait()
         vload(n).wait()
-
-        @pl.when(n == 3)
-        def _():
-            wload.start()
-            qload.start()
 
         for h in range(HEADS):
             col = slice(h * DH, (h + 1) * DH)
@@ -258,7 +256,7 @@
 
     exchange_z()
 
-    def near_attention(n, carry):
+    def attend(n):
         r = rows(n)
         w = wt[r, :]
         w16 = w.astype(BF)
@@ -302,9 +300,16 @@
                 stacked(beside(va, z_hi), beside(z_hi, vb), states),
             )
 
-        for at_n, hook in hooks:
-
-            @pl.when(n == at_n)
+    order = (2, 1, 3)
+
+    def offset(i):
+        return jnp.where(i == 0, order[0], jnp.where(i == 1, order[1], order[2]))
+
+    def attend_sent(i, carry):
+        attend(2 * plus(x, offset(lax.rem(i, 3))) + i // 3)
+        for at_i, hook in hooks:
+
+            @pl.when(i == at_i)
             def _():
                 hook()
 
@@ -318,31 +323,74 @@
 
     sources = (3, 1, 2)
 
-    def send_wz(es):
-        for e in es:
-            wx_a(plus(x, e), 1).wait_recv()
-            for d in (2, 1, 3):
-                wz(plus(x, e), z, d).start()
+    def half_a(quarter, p, k):
+        return wb.at[quarter, rows(2 * p + k, DH // 2), pl.ds(pl.multiple_of(c * 1024, 1024), 512)]
+
+    def half_b(quarter, p, k):
+        return wb.at[quarter, rows(2 * p + k, DH // 2), pl.ds(pl.multiple_of(c * 1024 + 512, 512), 512)]
+
+    def fz(quarter, p, k, d):
+        piece = half_a(quarter, p, k)
+        return rcopy(piece, piece, fz_s.at[quarter, k], fz_r.at[quarter, k], zpeer(plus(z, d)))
+
+    def fy(quarter, p, k, d):
+        piece = half_b(quarter, p, k)
+        return rcopy(piece, piece, fy_s.at[quarter, k], fy_r.at[quarter, k], ypeer(plus(y, d)))
+
+    def send_wz(e):
+        wx_a(plus(x, e), 1).wait_recv()
+        for d in (1, 3):
+            wz(plus(x, e), z, d).start()
+
+    def send_wy(e):
+        wx_b(plus(x, e), 1).wait_recv()
+        for d in (1, 3):
+            wy(plus(x, e), y, d).start()
+
+    def forward_z(e):
+        quarter = plus(x, e)
+        wz(quarter, plus(z, 3), 1).wait_recv()
+        fz(quarter, plus(z, 3), 0, 1).start()
+        wz(quarter, plus(z, 1), 3).wait_recv()
+        fz(quarter, plus(z, 1), 1, 3).start()
+
+    def forward_y(e):
+        quarter = plus(x, e)
+        wy(quarter, plus(y, 3), 1).wait_recv()
+        fy(quarter, plus(y, 3), 0, 1).start()
+        wy(quarter, plus(y, 1), 3).wait_recv()
+        fy(quarter, plus(y, 1), 1, 3).start()
+
+    def wd(quarter, e, part):
+        cols = pl.ds(pl.multiple_of(c * 1024 + part * 512, 512), 512)
+        piece = wb.at[quarter, :, cols]
+        return rcopy(piece, piece, wd_s.at[e - 1, part], wd_r.at[quarter, part], partner)
+
+    def share_a(e):
+        quarter = plus(x, e)
+        for k in range(2):
+            fz(quarter, plus(z, 2), k, 1 + 2 * k).wait_recv()
+        wd(quarter, e, 0).start()
+
+    def share_b(e):
+        quarter = plus(x, e)
+        for k in range(2):
+            fy(quarter, plus(y, 2), k, 1 + 2 * k).wait_recv()
+        wd(quarter, e, 1).start()
 
     hooks = (
-        (5, lambda: exchange_y(0)),
-        (7, lambda: exchange_y(1)),
+        (4, lambda: exchange_y(0)),
+        (5, lambda: exchange_y(1)),
     )
-    lax.fori_loop(0, NBLK, near_attention, 0)
-    send_wz((3, 1))
+    lax.fori_loop(0, 6, attend_sent, 0)
     exchange_end(0)
     exchange_end(1)
-    send_wz((2,))
-    for e in sources:
-        wx_b(plus(x, e), 1).wait_recv()
-        for d in (2, 1, 3):
-            wy(plus(x, e), y, d).start()
 
     def acopy(src, slot, d):
-        own = lax.rem(slot + c, 2)
+        mine = lax.rem(slot + c, 2)
         block = 2 * plus(src, d)
         if slot < 2:
-            cols = pl.ds(pl.multiple_of(own * 2 * DH, 2 * DH), 2 * DH)
+            cols = pl.ds(pl.multiple_of(mine * 2 * DH, 2 * DH), 2 * DH)
             here = nb.at[rows(block), cols]
             there = rb.at[src, pl.ds(0, BLK), cols]
         else:
@@ -361,11 +409,6 @@
             done.append((t * lax.rsqrt(ms + EPSILON)).astype(BF))
         nb[r, col] = beside(*done)
 
-    order = (2, 1, 3)
-
-    def offset(i):
-        return jnp.where(i == 0, order[0], jnp.where(i == 1, order[1], jnp.where(i == 2, order[2], 0)))
-
     def send_slots(i, slots):
         for m, d in enumerate(order):
 
@@ -390,44 +433,56 @@
         return carry
 
     early(0)
+    send_wz(3)
+    send_wz(1)
+    send_wy(3)
+    send_wy(1)
     for i in range(2):
         theirs = far_at(1 - c, i, 1, 4)
         rcopy(theirs, theirs, l_s.at[i], l_r.at[i], partner).wait_recv()
     early(1)
-    lax.fori_loop(0, 4, late, 0)
-    finish(2 * x, 0)
-    finish(2 * x, 1)
+    send_wz(2)
+    send_wy(2)
+    lax.fori_loop(0, 3, late, 0)
+    for e in sources:
+        forward_z(e)
+        forward_y(e)
+
+    def keep(i, carry):
+        attend(2 * x + i)
+        finish(2 * x + i, 0)
+        finish(2 * x + i, 1)
+        return carry
+
+    lax.fori_loop(0, 2, keep, 0)
 
     NC = 512
+
+    def project_own(i, carry):
+        cl = rows(i, NC)
+        own[:, cl] = dot(nb[rows(x, OROWS), :], wb[x, :, cl])
+        return carry
 
     def project(row, size):
         rws = pl.ds(row, size)
 
         def body(i, carry):
             cl = rows(i, NC)
-            s = dot(nb[pl.ds(pl.multiple_of(x * OROWS, OROWS) + row, size), :], wb[x, :, cl])
-            for e in sources:
+            s = dot(rb[plus(x, sources[0]), rws, :], wb[plus(x, sources[0]), :, cl])
+            for e in sources[1:]:
                 s = s + dot(rb[plus(x, e), rws, :], wb[plus(x, e), :, cl])
-            o_ref[rws, cl] = s.astype(BF)
+            o_ref[rws, cl] = (s + own[rws, cl]).astype(BF)
             return carry
 
         lax.fori_loop(0, OUT // NC, body, 0)
 
-    def half_of(quarter):
-        return wb.at[quarter, :, pl.ds(pl.multiple_of(c * 1024, 1024), 1024)]
-
-    def wd(quarter, e):
-        return rcopy(half_of(quarter), half_of(quarter), wd_s.at[e - 1], wd_r.at[quarter], partner)
-
     for e in sources:
-        quarter = plus(x, e)
-        for d in (1, 2, 3):
-            wz(quarter, plus(z, d), d).wait_recv()
-            wy(quarter, plus(y, d), d).wait_recv()
-        wd(quarter, e).start()
-
+        share_a(e)
+        share_b(e)
+    lax.fori_loop(0, OUT // NC, project_own, 0)
     for e in sources:
-        wd(plus(x, e), e).wait_recv()
+        for part in range(2):
+            wd(plus(x, e), e, part).wait_recv()
     for slot in range(4):
         for e in sources:
             acopy(plus(x, e), slot, RING - e).wait_recv()
@@ -450,10 +505,12 @@
         wx_a(x, d).wait_send()
         wx_b(x, d).wait_send()
         quarter = plus(x, d)
-        for dd in (1, 2, 3):
+        for k, dd in ((0, 1), (1, 3)):
             wz(quarter, z, dd).wait_send()
             wy(quarter, y, dd).wait_send()
-        wd(quarter, d).wait_send()
+            fz(quarter, plus(z, dd), k, dd).wait_send()
+            fy(quarter, plus(y, dd), k, dd).wait_send()
+            wd(quarter, d, k).wait_send()
         for slot in range(4):
             acopy(x, slot, d).wait_send()
 
@@ -482,10 +539,12 @@
         pltpu.VMEM((TOK, HEADS * REMOTE * DH), BF),
         pltpu.VMEM((TOK, COLS), BF),
         pltpu.VMEM((RING, OROWS, COLS), BF),
+        pltpu.VMEM((OROWS, OUT), F32),
         dma((2, NBLK)), dma, dma,
         dma, dma, dma((3, 2)), dma((RING, 2)), dma((3, 2)), dma((RING, 2)), dma((2,)), dma((2,)),
         dma((3, 2)), dma((RING, 2)), dma((RING, 3)), dma((RING, RING)), dma((RING, 3)), dma((RING, RING)),
-        dma((3,)), dma((RING,)), dma((3, 4)), dma((RING, 4)),
+        dma((RING, 2)), dma((RING, 2)), dma((RING, 2)), dma((RING, 2)),
+        dma((3, 2)), dma((RING, 2)), dma((3, 4)), dma((RING, 4)),
     ]
     return pl.pallas_call(
         kernel,

time: 52.4 us -> 49.4 us (0.943)
  Pallas kernels: 50.9 us -> 47.9 us
    pallas_call x1, Pallas kernels: 50.9 us -> 47.9 us  [body(): pl.pallas_call(kernel, out_shape=pltpu.VMEM((OROWS, OUT), BF), in_specs=[...]
where the time goes in v4:
time: 49.4 us; the launch traced here: 49.2 us
  Pallas kernels  47.9 us (97%)
  local copies, waits for them, and re-layouts  1.32 us (3%)
    pallas_call x1, Pallas kernels, body(): pl.pallas_call(kernel, out_shape=pltpu.VMEM((OROWS, OUT), BF), in_specs=[...  47.9 us
    unnamed x1, local copies, waits for them, and re-layouts  1.32 us

profile of v4, /device:TPU:1, one launch (start us, length us, event | category | flops | bytes accessed | tf_op | source)
XLA Modules:
  0.0 49.2 jit_solution(17148151486441757117)
XLA Ops:
  0.0 47.9 %shard_map.64 = bf16[512,2048]{1,0:T(8,128)(2,1)S(1)} custom-call(s32[16,128]{1,0:T(8,128)} %bitcast.1, f32[16,4,20]{2,1,0:T(4,128)} %tab_ref.1, bf16[2048,512]{1,0:T(8,128)(2,1)} %q_hbm.1, bf16[2048,512]{1,0:T(8,128)(2,1)} %k_hbm.1, bf16[2048,512]{1,0:T(8,128)(2,1)} %v_hbm.1, bf16[512,2048]{1,0:T(8,128)(2,1)} %w_hbm.1), custom_call_target="tpu_custom_call" | custom-call | tf_op jit(solution)/shard_map/pallas_call | solution.py:549
  47.9 1.3 %copy.8 = bf16[512,2048]{1,0:T(8,128)(2,1)} copy(bf16[512,2048]{1,0:T(8,128)(2,1)S(1)} %shard_map.64) | data formatting | bytes 4194304

commit v5 on v4

--- a/solution.py
+++ b/solution.py
@@ -380,7 +380,7 @@
 
     hooks = (
         (4, lambda: exchange_y(0)),
-        (5, lambda: exchange_y(1)),
+        (5, lambda: (exchange_y(1), send_wz(3), send_wz(1))),
     )
     lax.fori_loop(0, 6, attend_sent, 0)
     exchange_end(0)
@@ -432,11 +432,9 @@
         send_slots(i, (2, 3))
         return carry
 
-    early(0)
-    send_wz(3)
-    send_wz(1)
     send_wy(3)
     send_wy(1)
+    early(0)
     for i in range(2):
         theirs = far_at(1 - c, i, 1, 4)
         rcopy(theirs, theirs, l_s.at[i], l_r.at[i], partner).wait_recv()
@@ -444,14 +442,22 @@
     send_wz(2)
     send_wy(2)
     lax.fori_loop(0, 3, late, 0)
-    for e in sources:
-        forward_z(e)
-        forward_y(e)
+    forward_z(3)
+    forward_y(3)
+    forward_z(1)
 
     def keep(i, carry):
         attend(2 * x + i)
         finish(2 * x + i, 0)
         finish(2 * x + i, 1)
+
+        @pl.when(i == 0)
+        def _():
+            forward_y(1)
+            forward_z(2)
+            share_a(3)
+            share_b(3)
+
         return carry
 
     lax.fori_loop(0, 2, keep, 0)
@@ -476,20 +482,29 @@
 
         lax.fori_loop(0, OUT // NC, body, 0)
 
-    for e in sources:
-        share_a(e)
-        share_b(e)
-    lax.fori_loop(0, OUT // NC, project_own, 0)
-    for e in sources:
+    def share_done(e):
         for part in range(2):
             wd(plus(x, e), e, part).wait_recv()
-    for slot in range(4):
-        for e in sources:
+
+    def arrived(slot, es):
+        for e in es:
             acopy(plus(x, e), slot, RING - e).wait_recv()
-        if slot == 1:
-            project(0, BLK)
-        elif slot > 1:
-            project(slot * HALF, HALF)
+
+    forward_y(2)
+    share_a(1)
+    share_b(1)
+    lax.fori_loop(0, OUT // NC, project_own, 0)
+    share_a(2)
+    share_b(2)
+    share_done(3)
+    share_done(1)
+    share_done(2)
+    arrived(0, sources)
+    arrived(1, sources)
+    project(0, BLK)
+    for slot in (2, 3):
+        arrived(slot, sources)
+        project(slot * HALF, HALF)
 
     tcopy.wait_send()
     for i in range(2):

time: 49.4 us -> 48.4 us (0.980)
  Pallas kernels: 47.9 us -> 46.4 us
    pallas_call x1, Pallas kernels: 47.9 us -> 46.4 us  [body(): pl.pallas_call(kernel, out_shape=pltpu.VMEM((OROWS, OUT), BF), in_specs=[...]
where the time goes in v5:
time: 48.4 us; the launch traced here: 47.8 us
  Pallas kernels  46.4 us (96%)
  local copies, waits for them, and re-layouts  1.32 us (3%)
    pallas_call x1, Pallas kernels, body(): pl.pallas_call(kernel, out_shape=pltpu.VMEM((OROWS, OUT), BF), in_specs=[...  46.4 us
    unnamed x1, local copies, waits for them, and re-layouts  1.32 us

profile of v5, /device:TPU:1, one launch (start us, length us, event | category | flops | bytes accessed | tf_op | source)
XLA Modules:
  0.0 47.8 jit_solution(17350110339169465303)
XLA Ops:
  0.0 46.4 %shard_map.64 = bf16[512,2048]{1,0:T(8,128)(2,1)S(1)} custom-call(s32[16,128]{1,0:T(8,128)} %bitcast.1, f32[16,4,20]{2,1,0:T(4,128)} %tab_ref.1, bf16[2048,512]{1,0:T(8,128)(2,1)} %q_hbm.1, bf16[2048,512]{1,0:T(8,128)(2,1)} %k_hbm.1, bf16[2048,512]{1,0:T(8,128)(2,1)} %v_hbm.1, bf16[512,2048]{1,0:T(8,128)(2,1)} %w_hbm.1), custom_call_target="tpu_custom_call" | custom-call | tf_op jit(solution)/shard_map/pallas_call | solution.py:564
  46.4 1.3 %copy.8 = bf16[512,2048]{1,0:T(8,128)(2,1)} copy(bf16[512,2048]{1,0:T(8,128)(2,1)S(1)} %shard_map.64) | data formatting | bytes 4194304

commit v6 on v5

--- a/solution.py
+++ b/solution.py
@@ -379,8 +379,8 @@
         wd(quarter, e, 1).start()
 
     hooks = (
-        (4, lambda: exchange_y(0)),
-        (5, lambda: (exchange_y(1), send_wz(3), send_wz(1))),
+        (3, lambda: exchange_y(0)),
+        (4, lambda: exchange_y(1)), (5, lambda: (send_wz(3), send_wz(1))),
     )
     lax.fori_loop(0, 6, attend_sent, 0)
     exchange_end(0)
@@ -469,15 +469,19 @@
         own[:, cl] = dot(nb[rows(x, OROWS), :], wb[x, :, cl])
         return carry
 
-    def project(row, size):
+    def project(row, size, es=sources, last=True):
         rws = pl.ds(row, size)
 
         def body(i, carry):
             cl = rows(i, NC)
-            s = dot(rb[plus(x, sources[0]), rws, :], wb[plus(x, sources[0]), :, cl])
-            for e in sources[1:]:
+            s = dot(rb[plus(x, es[0]), rws, :], wb[plus(x, es[0]), :, cl])
+            for e in es[1:]:
                 s = s + dot(rb[plus(x, e), rws, :], wb[plus(x, e), :, cl])
-            o_ref[rws, cl] = (s + own[rws, cl]).astype(BF)
+            s = s + own[rws, cl]
+            if last:
+                o_ref[rws, cl] = s.astype(BF)
+            else:
+                own[rws, cl] = s
             return carry
 
         lax.fori_loop(0, OUT // NC, body, 0)
@@ -502,9 +506,12 @@
     arrived(0, sources)
     arrived(1, sources)
     project(0, BLK)
-    for slot in (2, 3):
-        arrived(slot, sources)
-        project(slot * HALF, HALF)
+    arrived(2, sources)
+    project(2 * HALF, HALF)
+    arrived(3, (2,))
+    project(3 * HALF, HALF, (2,), False)
+    arrived(3, (3, 1))
+    project(3 * HALF, HALF, (3, 1))
 
     tcopy.wait_send()
     for i in range(2):

time: 48.4 us -> 47.6 us (0.983); the launches traced: 47.8 us -> 47.4 us
  no operation moved by 1% of the time
where the time goes in v6:
time: 47.6 us; the launch traced here: 47.4 us
  Pallas kernels  46.1 us (97%)
  local copies, waits for them, and re-layouts  1.32 us (3%)
    pallas_call x1, Pallas kernels, body(): pl.pallas_call(kernel, out_shape=pltpu.VMEM((OROWS, OUT), BF), in_specs=[...  46.1 us
    unnamed x1, local copies, waits for them, and re-layouts  1.32 us

profile of v6, /device:TPU:1, one launch (start us, length us, event | category | flops | bytes accessed | tf_op | source)
XLA Modules:
  0.0 47.4 jit_solution(3853696532666757599)
XLA Ops:
  0.0 46.1 %shard_map.64 = bf16[512,2048]{1,0:T(8,128)(2,1)S(1)} custom-call(s32[16,128]{1,0:T(8,128)} %bitcast.1, f32[16,4,20]{2,1,0:T(4,128)} %tab_ref.1, bf16[2048,512]{1,0:T(8,128)(2,1)} %q_hbm.1, bf16[2048,512]{1,0:T(8,128)(2,1)} %k_hbm.1, bf16[2048,512]{1,0:T(8,128)(2,1)} %v_hbm.1, bf16[512,2048]{1,0:T(8,128)(2,1)} %w_hbm.1), custom_call_target="tpu_custom_call" | custom-call | tf_op jit(solution)/shard_map/pallas_call | solution.py:571
  46.1 1.3 %copy.8 = bf16[512,2048]{1,0:T(8,128)(2,1)} copy(bf16[512,2048]{1,0:T(8,128)(2,1)S(1)} %shard_map.64) | data formatting | bytes 4194304

commit v7 on v6

--- a/solution.py
+++ b/solution.py
@@ -120,8 +120,7 @@
     for n in range(NBLK):
         kload(n).start()
         vload(n).start()
-        if n == 3:
-            wload.start()
+    wload.start()
     qload.start()
 
     def leaf_body(n, carry):
@@ -462,7 +461,7 @@
 
     lax.fori_loop(0, 2, keep, 0)
 
-    NC = 512
+    NC = 1024
 
     def project_own(i, carry):
         cl = rows(i, NC)

time: 47.6 us -> 47.2 us (level)
  no operation moved by 1% of the time
where the time goes in v7:
time: 47.2 us; the launch traced here: 47.1 us
  Pallas kernels  45.7 us (97%)
  local copies, waits for them, and re-layouts  1.32 us (3%)
    pallas_call x1, Pallas kernels, body(): pl.pallas_call(kernel, out_shape=pltpu.VMEM((OROWS, OUT), BF), in_specs=[...  45.7 us
    unnamed x1, local copies, waits for them, and re-layouts  1.32 us

profile of v7, /device:TPU:1, one launch (start us, length us, event | category | flops | bytes accessed | tf_op | source)
XLA Modules:
  0.0 47.1 jit_solution(8406715958095574720)
XLA Ops:
  0.0 45.7 %shard_map.64 = bf16[512,2048]{1,0:T(8,128)(2,1)S(1)} custom-call(s32[16,128]{1,0:T(8,128)} %bitcast.1, f32[16,4,20]{2,1,0:T(4,128)} %tab_ref.1, bf16[2048,512]{1,0:T(8,128)(2,1)} %q_hbm.1, bf16[2048,512]{1,0:T(8,128)(2,1)} %k_hbm.1, bf16[2048,512]{1,0:T(8,128)(2,1)} %v_hbm.1, bf16[512,2048]{1,0:T(8,128)(2,1)} %w_hbm.1), custom_call_target="tpu_custom_call" | custom-call | tf_op jit(solution)/shard_map/pallas_call | solution.py:570
  45.8 1.3 %copy.8 = bf16[512,2048]{1,0:T(8,128)(2,1)} copy(bf16[512,2048]{1,0:T(8,128)(2,1)S(1)} %shard_map.64) | data formatting | bytes 4194304
